TPU v7x, 32 devices: a whole 2x2x4 slice. The times are simulated.
32 devices in a mesh: grp: 4 (over y, x), dev: 8 (over z, core).
Axes of the slice: x: 2, y: 2, z: 4, core: 2. Of those that a mesh axis runs over, the one named last changes fastest.
Arguments:
- token_ids: int32 [128, 128], P(('grp', 'dev')), may hold values from 0 to 128255, as said below
- sensitivity: bfloat16 [128, 128, 4096], P(('grp', 'dev')), may hold values from -6 to 6
- last_hidden: bfloat16 [128, 4096], P(('grp', 'dev')), may hold values from -6 to 6
- lengths: int32 [128], P(('grp', 'dev')), may hold values from 97 to 128
- norm_gain: float32 [4096], replicated, may hold values from 0.25 to 1.75
- reward_head: float32 [4096], replicated, may hold values from -0.09375 to 0.09375
- chosen_index: int32 [64], replicated, may hold values from 0 to 127, as said below
- rejected_index: int32 [64], replicated, may hold values from 0 to 127, as said below
- shard_owner: int32 [32], replicated, may hold values from 0 to 31, each once
Outputs:
- owned_grad: bfloat16 [128256, 4096], P(('grp', 'dev'))
- head_grad: float32 [4096], P(('grp', 'dev'))
Inputs may be any that keep to these rules, and one draw needn't show every extreme that they name: `token_ids`: within the token slots of one device, at most 32 ids fall in any one vocabulary shard of 4008 rows, and on every device some shard gets exactly 32. chosen_index and rejected_index together name every response exactly once. `rejected_index`: see chosen_index.
All inputs are finite; a program needn't handle non-finite values.
Results may differ from a plain program's by a relative error of at most 0.0042.
Values may be sent and summed in bfloat16 or wider, within the bound.
A program may use at most 128 MiB of HBM per device.

v0:
```python
import functools

import jax
import jax.numpy as jnp
from jax import lax
from jax.experimental import pallas as pl
from jax.experimental.pallas import tpu as pltpu
from jax.sharding import PartitionSpec as P

VOCAB = 128256
MESH = pl.DeviceIdType.MESH


def exchange_kernel(n, n_dev, meta_ref, rows_ref, meta_out, rows_out, send_sem, recv_sem, own_sem):
    me = lax.axis_index("grp") * n_dev + lax.axis_index("dev")

    def coord(t):
        return (t // n_dev, lax.rem(t, n_dev))

    barrier = pltpu.get_barrier_semaphore()

    def greet(k, c):
        t = lax.rem(me + k, n)
        pl.semaphore_signal(barrier, inc=1, device_id=coord(t), device_id_type=MESH)
        return c

    lax.fori_loop(1, n, greet, 0)
    own = [
        pltpu.make_async_copy(src.at[me], dst.at[me], own_sem.at[i])
        for i, (src, dst) in enumerate(((meta_ref, meta_out), (rows_ref, rows_out)))
    ]
    for c in own:
        c.start()
    pl.semaphore_wait(barrier, n - 1)

    def copies(src_block, dst_block, to):
        return [
            pltpu.make_async_remote_copy(
                src_ref=src.at[src_block],
                dst_ref=dst.at[dst_block],
                send_sem=send_sem.at[i, src_block],
                recv_sem=recv_sem.at[i, dst_block],
                device_id=coord(to),
                device_id_type=MESH,
            )
            for i, (src, dst) in enumerate(((meta_ref, meta_out), (rows_ref, rows_out)))
        ]

    def send(k, c):
        t = lax.rem(me + k, n)
        for cp in copies(t, me, t):
            cp.start()
        return c

    lax.fori_loop(1, n, send, 0)

    def finish(k, c):
        t = lax.rem(me + k, n)
        for cp in copies(t, me, t):
            cp.wait_send()
        s = lax.rem(me + n - k, n)
        for cp in copies(s, s, s):
            cp.wait_recv()
        return c

    lax.fori_loop(1, n, finish, 0)
    for c in own:
        c.wait()


def exchange(meta, rows, n, n_dev):
    anyspec = pl.BlockSpec(memory_space=pl.ANY)
    return pl.pallas_call(
        functools.partial(exchange_kernel, n, n_dev),
        out_shape=(
            jax.ShapeDtypeStruct(meta.shape, meta.dtype),
            jax.ShapeDtypeStruct(rows.shape, rows.dtype),
        ),
        in_specs=[anyspec, anyspec],
        out_specs=(anyspec, anyspec),
        scratch_shapes=[
            pltpu.SemaphoreType.DMA((2, n)),
            pltpu.SemaphoreType.DMA((2, n)),
            pltpu.SemaphoreType.DMA((2,)),
        ],
        compiler_params=pltpu.CompilerParams(collective_id=0, has_side_effects=True),
    )(meta, rows)


def local(
    token_ids,
    sensitivity,
    last_hidden,
    lengths,
    norm_gain,
    reward_head,
    chosen_index,
    rejected_index,
    shard_owner,
):
    resp_local, block_len = token_ids.shape
    width = sensitivity.shape[2]
    tok_local = resp_local * block_len
    n_dev = lax.axis_size("dev")
    devices = shard_owner.shape[0]
    responses = devices * resp_local
    shard_rows = VOCAB // devices
    capacity = max(2, (2 * tok_local + devices - 1) // devices)
    cols = width // devices
    lanes = -(-max(cols, capacity, resp_local) // 128) * 128
    hidden = last_hidden.astype(jnp.float32)
    normed = (
        hidden / jnp.sqrt(jnp.mean(hidden * hidden, axis=-1, keepdims=True) + 1e-05) * norm_gain
    )
    own_reward = jnp.sum(normed * reward_head, axis=-1)

    positions = jnp.arange(block_len, dtype=jnp.int32)
    live = (positions[None, :] < lengths[:, None]).reshape(tok_local)
    ids = token_ids.reshape(tok_local)
    shard_of = ids // shard_rows
    offset = ids - shard_of * shard_rows
    shard_hot = shard_of[:, None] == jnp.arange(devices, dtype=jnp.int32)[None, :]
    owner = jnp.sum(jnp.where(shard_hot, shard_owner[None, :], 0), axis=1)
    live_hot = (shard_hot & live[:, None]).astype(jnp.bfloat16)
    token_pos = jnp.arange(tok_local, dtype=jnp.int32)
    earlier = (token_pos[:, None] > token_pos[None, :]).astype(jnp.bfloat16)
    before = jnp.dot(earlier, live_hot, preferred_element_type=jnp.float32)
    rank = jnp.sum(before * live_hot.astype(jnp.float32), axis=1).astype(jnp.int32)
    slot = jnp.where(live, owner * capacity + rank, -1)
    slot_match = slot[None, :] == jnp.arange(devices * capacity, dtype=jnp.int32)[:, None]
    outgoing = jnp.dot(
        slot_match.astype(jnp.bfloat16),
        sensitivity.reshape(tok_local, width),
        preferred_element_type=jnp.float32,
    ).astype(jnp.bfloat16)
    code = (offset + 1) * resp_local + token_pos // block_len
    codes = jnp.sum(jnp.where(slot_match, code[None, :], 0), axis=1)
    codes = codes.reshape(devices, capacity)
    target_out = codes // resp_local - 1
    resp_out = codes - codes // resp_local * resp_local

    def lane_pad(a):
        return jnp.pad(a, ((0, 0), (0, lanes - a.shape[1])))[:, None, :]

    normed_blocks = normed.reshape(resp_local, devices, cols).transpose(1, 0, 2)
    meta = jnp.concatenate(
        [
            lane_pad(target_out.astype(jnp.float32)),
            lane_pad(resp_out.astype(jnp.float32)),
            lane_pad(jnp.broadcast_to(own_reward[None, :], (devices, resp_local))),
            jnp.zeros((devices, 1, lanes), jnp.float32),
            jnp.pad(normed_blocks, ((0, 0), (0, 0), (0, lanes - cols))),
        ],
        axis=1,
    )
    extra = -meta.shape[1] % 8
    meta = jnp.pad(meta, ((0, 0), (0, extra), (0, 0)))
    meta_in, arrived = exchange(
        meta, outgoing.reshape(devices, capacity, width), devices, n_dev
    )

    targets = meta_in[:, 0, :capacity].astype(jnp.int32).reshape(devices * capacity)
    resp_in = meta_in[:, 1, :capacity].astype(jnp.int32)
    reward = meta_in[:, 2, :resp_local].reshape(responses)
    normed_in = meta_in[:, 4 : 4 + resp_local, :cols]
    all_resp = jnp.arange(responses, dtype=jnp.int32)
    sign_table = (chosen_index[:, None] == all_resp[None, :]).astype(jnp.float32) - (
        rejected_index[:, None] == all_resp[None, :]
    ).astype(jnp.float32)
    margin = jnp.sum(sign_table * reward[None, :], axis=1)
    push = -jax.nn.sigmoid(-margin)
    reward_grad = jnp.sum(sign_table * push[:, None], axis=0).reshape(devices, resp_local)
    head_grad = jnp.sum(reward_grad[:, :, None] * normed_in, axis=(0, 1))
    resp_hot = resp_in[:, :, None] == jnp.arange(resp_local, dtype=jnp.int32)[None, None, :]
    scale = jnp.sum(jnp.where(resp_hot, reward_grad[:, None, :], 0.0), axis=2)
    total = devices * capacity
    scale = scale.reshape(total)
    rows_in = arrived.reshape(total, width)

    def place_all(operands):
        rows, targets, scale = operands
        scaled = (scale[:, None] * rows).astype(jnp.bfloat16)
        placing = (targets[None, :] == jnp.arange(shard_rows, dtype=jnp.int32)[:, None]).astype(
            jnp.bfloat16
        )
        return jnp.dot(placing, scaled, preferred_element_type=jnp.float32).astype(jnp.bfloat16)

    operands = (rows_in, targets, scale)
    blocks, window = 3, total // 4
    if shard_rows % (8 * blocks) or window % 128:
        owned = place_all(operands)
        return (owned, head_grad)
    block_rows = shard_rows // blocks
    first_row = jnp.arange(blocks, dtype=jnp.int32) * block_rows
    in_block = (targets[:, None] >= first_row[None, :]) & (
        targets[:, None] < first_row[None, :] + block_rows
    )
    block_hot = in_block.astype(jnp.bfloat16)
    pos = jnp.arange(total, dtype=jnp.int32)
    ahead = (pos[:, None] > pos[None, :]).astype(jnp.bfloat16)
    rank_in = jnp.dot(ahead, block_hot, preferred_element_type=jnp.float32).astype(jnp.int32)
    slot_base = jnp.arange(blocks, dtype=jnp.int32) * window
    packed_slot = jnp.sum(jnp.where(in_block, rank_in + slot_base[None, :] + 1, 0), axis=1) - 1
    fits = jnp.max(jnp.sum(in_block.astype(jnp.int32), axis=0)) <= window

    def place_packed(operands):
        rows, targets, scale = operands
        pack = packed_slot[None, :] == jnp.arange(blocks * window, dtype=jnp.int32)[:, None]
        packed_scale = jnp.sum(jnp.where(pack, scale[None, :], 0.0), axis=1)
        packed_target = jnp.sum(jnp.where(pack, targets[None, :] + 1, 0), axis=1) - 1
        packed = jnp.dot(pack.astype(jnp.bfloat16), rows, preferred_element_type=jnp.float32)
        packed = (packed_scale[:, None] * packed).astype(jnp.bfloat16)
        row_of = first_row[:, None] + jnp.arange(block_rows, dtype=jnp.int32)[None, :]
        placing = packed_target.reshape(blocks, 1, window) == row_of[:, :, None]
        owned = lax.dot_general(
            placing.astype(jnp.bfloat16),
            packed.reshape(blocks, window, width),
            (((2,), (1,)), ((0,), (0,))),
            preferred_element_type=jnp.float32,
        )
        return owned.astype(jnp.bfloat16).reshape(shard_rows, width)

    owned = lax.cond(fits, place_packed, place_all, operands)
    return (owned, head_grad)


def solution(mesh):
    placed = (
        P(("grp", "dev"), None),
        P(("grp", "dev"), None, None),
        P(("grp", "dev"), None),
        P(("grp", "dev")),
        P(),
        P(),
        P(),
        P(),
        P(),
    )
    return jax.shard_map(
        local,
        mesh=mesh,
        in_specs=placed,
        out_specs=(P(("grp", "dev"), None), P(("grp", "dev"))),
        check_vma=False,
    )
```

profile of v0, /device:TPU:11, one launch (start us, length us, event | category | flops | bytes accessed | tf_op | source)
XLA Modules:
  0.0 251.3 jit_solution(8812491330006134046)
XLA Ops:
  0.6 0.9 fusion.11
  1.5 0.7 fusion.27
  2.3 0.7 add_select_fusion.2
  3.0 0.3 fusion.7
  3.3 0.7 select_reduce_fusion.5
  4.0 0.7 add_select_fusion.3
  4.7 0.3 select_reduce_fusion.3
  5.2 1.0 fusion.30
  6.2 0.8 concatenate.3.meta_ref
  7.0 8.9 %convolution_convert_fusion.2 = bf16[1024,4096]{1,0:T(8,128)(2,1)} fusion(bf16[512,4096]{1,0:T(8,128)(2,1)} %bitcast.57, s32[512]{0:T(512)S(1)} %add_select_fusion.3), kind=kOutput, calls=%fused_computation.21 | convolution fusion | flops 4299685888 | bytes 12584960 | tf_op jit(solution)/shard_map/dot_general | solution.py:131
  15.8 197.5 %shard_map.104 = (f32[32,8,128]{2,1,0:T(8,128)}, bf16[32,32,4096]{2,1,0:T(8,128)(2,1)}) custom-call(f32[32,8,128]{2,1,0:T(8,128)} %concatenate.3.meta_ref, bf16[32,32,4096]{2,1,0:T(8,128)(2,1)} %bitcast.48), custom_call_target="tpu_custom_call" | custom-call | tf_op jit(solution)/shard_map/pallas_call | solution.py:73
  213.4 1.0 slice_reduce_fusion
  214.4 0.2 multiply_reduce_fusion.3
  214.9 1.5 multiply_reduce_fusion
  216.5 1.0 fusion.29
  217.4 1.0 slice_convert_fusion
  218.5 0.2 convert_reduce_fusion
  218.7 0.6 reduce_max.9
  220.1 0.5 fusion.8
  220.6 30.7 %conditional.1 = (bf16[4008,4096]{1,0:T(8,128)(2,1)}) conditional(s32[]{:T(128)} %convert_element_type.100, (s32[32,32]{1,0:T(8,128)S(1)}, f32[32,32]{1,0:T(8,128)S(1)}, bf16[1024,4096]{1,0:T(8,128)(2,1)}) %tuple.27, (s32[1,3]{1,0:T(1,128)S(1)}, s32[1024,3]{0,1:T(4,128)S(1)}, pred[1024,3]{0,1:T(4,128)(4,1)S(1)}, s32[32,32]{1,0:T(8,128)S(1)}, ...), branch_computations={%region_10.11_spmd, %region_11.15_spmd} | conditional | flops 33654644736 | bytes 53934480 | solution.py:223
  220.9 0.4 select_reduce_fusion
  221.3 12.0 %multiply_convert_fusion.2 = bf16[768,4096]{1,0:T(8,128)(2,1)} fusion(bf16[1024,4096]{1,0:T(8,128)(2,1)} %get-tuple-element.52, f32[768]{0:T(1024)S(1)} %select_reduce_fusion, s32[1024]{0:T(1024)S(1)} %broadcast_add_fusion.2), kind=kOutput, calls=%fused_computation.6 | convolution fusion | flops 6449528832 | bytes 14687232 | tf_op jit(solution)/shard_map/cond/branch_1_fun/dot_general | solution.py:211
  233.3 0.4 select_reduce_fusion.1
  233.8 17.4 %convolution_convert_fusion.1 = bf16[3,1336,4096]{2,1,0:T(8,128)(2,1)} fusion(bf16[3,256,4096]{2,1,0:T(8,128)(2,1)} %bitcast.49, s32[3,1336]{1,0:T(4,128)S(1)} %iota_add_fusion, s32[3,256]{1,0:T(4,128)S(1)} %sub.36), kind=kOutput, calls=%fused_computation.5 | convolution fusion | flops 8422828032 | bytes 39144096 | tf_op jit(solution)/shard_map/cond/branch_1_fun/dot_general | solution.py:215
  (32 shorter events, 1.1 us)
Async XLA Ops:
  15.8 198.6 %copy-start = (s32[64]{0:T(128)S(1)}, s32[64]{0:T(128)}, u32[]{:S(2)}) copy-start(s32[64]{0:T(128)} %param.18) | copy-start | bytes 772
  15.8 198.6 %copy-start.1 = (s32[64]{0:T(128)S(1)}, s32[64]{0:T(128)}, u32[]{:S(2)}) copy-start(s32[64]{0:T(128)} %param.17) | copy-start | bytes 772
where the time goes:
time: 252 us; the launch traced here: 251 us
  Pallas kernels  198 us (79%)
  matrix products  39 us (15%)
  other arithmetic  10.8 us (4%)
    pallas_call x1, Pallas kernels, exchange(): pl.pallas_call(functools.partial(exchange_kernel, n, n_dev), out_shape=(j...  198 us
    dot_general x1, matrix products, place_packed(): lax.dot_general(placing.astype(jnp.bfloat16), packed.reshape(blocks, wind...  17.4 us
    dot_general x1, matrix products, place_packed(): jnp.dot(pack.astype(jnp.bfloat16), rows, preferred_element_type=jnp.float32)  12 us
    dot_general x1, matrix products, local(): jnp.dot(slot_match.astype(jnp.bfloat16), sensitivity.reshape(tok_local, w...  8.89 us

commit v1 on v0

--- a/solution.py
+++ b/solution.py
@@ -83,31 +83,285 @@
             pltpu.SemaphoreType.DMA((2, n)),
             pltpu.SemaphoreType.DMA((2,)),
         ],
+        compiler_params=pltpu.CompilerParams(collective_id=1, has_side_effects=True),
+    )(meta, rows)
+
+
+GROUP = 8
+NEAR = 32
+FAR = 16
+FWD = 8
+
+
+def relay_kernel(n_grp, n_dev, fm_ref, slots_ref, pmeta_ref, fm_out, rows_out, fmeta_out,
+                 pin, pmeta_in, fwd, fwd_meta, fm_sems, near_sems, far_sems, piece_sems,
+                 pm_sems, fwd_sems, fwdm_sems, own_sems):
+    g = lax.axis_index("grp")
+    v = lax.axis_index("dev")
+    hd = n_dev // 2
+    local_n = n_grp * hd
+    half = v // hd
+    u = lax.rem(v, hd)
+    me = g * n_dev + v
+    me_local = g * hd + u
+    n = n_grp * n_dev
+    pieces = n_grp + 1
+    near_g, far_g = NEAR // GROUP, FAR // GROUP
+    far_base = local_n * near_g
+    piece_base = far_base + local_n * far_g
+    fwd_base = piece_base
+    other = 1 - half
+
+    def coord(t):
+        return (t // n_dev, lax.rem(t, n_dev))
+
+    barrier = pltpu.get_barrier_semaphore()
+
+    def greet(k, c):
+        pl.semaphore_signal(
+            barrier, inc=1, device_id=coord(lax.rem(me + k, n)), device_id_type=MESH
+        )
+        return c
+
+    lax.fori_loop(1, n, greet, 0)
+
+    def local_copy(src, dst, i):
+        return pltpu.make_async_copy(src, dst, own_sems.at[i])
+
+    own = [
+        local_copy(fm_ref.at[me], fm_out.at[me], 0),
+        local_copy(
+            slots_ref.at[pl.ds(me_local * near_g, near_g)],
+            rows_out.at[pl.ds(me_local * near_g, near_g)],
+            1,
+        ),
+    ]
+    for cp in own:
+        cp.start()
+    pl.semaphore_wait(barrier, n - 1)
+
+    def remote(src, dst, send_sem, recv_sem, to):
+        return pltpu.make_async_remote_copy(
+            src_ref=src,
+            dst_ref=dst,
+            send_sem=send_sem,
+            recv_sem=recv_sem,
+            device_id=to,
+            device_id_type=MESH,
+        )
+
+    def piece_target(q):
+        if q < n_grp:
+            return (lax.rem(g + q, n_grp), other * hd + u)
+        return (g, other * hd + lax.rem(u + hd // 2, hd))
+
+    piece_copies = []
+    for q in range(pieces):
+        to = piece_target(q)
+        piece_copies.append(
+            remote(slots_ref.at[piece_base + q], pin.at[q],
+                   piece_sems.at[0, q], piece_sems.at[1, q], to)
+        )
+        piece_copies.append(
+            remote(pmeta_ref.at[q], pmeta_in.at[q], pm_sems.at[0, q], pm_sems.at[1, q], to)
+        )
+    for cp in piece_copies:
+        cp.start()
+
+    def fm_copy(src, dst, k):
+        return remote(fm_ref.at[src], fm_out.at[dst], fm_sems.at[0, k], fm_sems.at[1, k],
+                      coord(src))
+
+    def split(k):
+        a = k // hd
+        b = lax.rem(k, hd)
+        return a, b
+
+    def near_copy(k):
+        a, b = split(k)
+        tg, tu = lax.rem(g + a, n_grp), lax.rem(u + b, hd)
+        t = tg * hd + tu
+        return remote(
+            slots_ref.at[pl.ds(t * near_g, near_g)],
+            rows_out.at[pl.ds(me_local * near_g, near_g)],
+            near_sems.at[0, k],
+            near_sems.at[1, k],
+            (tg, half * hd + tu),
+        )
+
+    def far_copy(k):
+        a, b = split(k)
+        tg, tu = lax.rem(g + a, n_grp), lax.rem(u + b, hd)
+        t = tg * hd + tu
+        return remote(
+            slots_ref.at[pl.ds(far_base + t * far_g, far_g)],
+            rows_out.at[pl.ds(far_base + me_local * far_g, far_g)],
+            far_sems.at[0, k],
+            far_sems.at[1, k],
+            (tg, other * hd + tu),
+        )
+
+    def send_fm(k, c):
+        fm_copy(lax.rem(me + k, n), me, k).start()
+        return c
+
+    lax.fori_loop(1, n, send_fm, 0)
+
+    def send_far(k, c):
+        far_copy(k).start()
+        return c
+
+    def send_near(k, c):
+        near_copy(k).start()
+        return c
+
+    lax.fori_loop(0, local_n, send_far, 0)
+
+    for cp in piece_copies:
+        cp.wait_recv()
+    count = pieces * GROUP
+    marks = pmeta_in[...].reshape(count, 128)
+    used = marks[:, 0:1] > 0.0
+    dst = (marks[:, 1:2] * hd + marks[:, 2:3]).astype(jnp.int32)
+    lane = lax.broadcasted_iota(jnp.int32, (count, 128), 1)
+    hot = jnp.where((lane == dst) & used, 1.0, 0.0)
+    row_i = lax.broadcasted_iota(jnp.int32, (count, count), 0)
+    col_i = lax.broadcasted_iota(jnp.int32, (count, count), 1)
+    earlier = jnp.where(row_i > col_i, 1.0, 0.0)
+    before = jnp.dot(earlier, hot, preferred_element_type=jnp.float32)
+    rank = jnp.sum(before * hot, axis=1, keepdims=True).astype(jnp.int32)
+    slot = jnp.where(used & (rank < FWD), dst * FWD + rank, -1)
+    place = jnp.where(lane == slot, 1.0, 0.0)
+    contract = (((0,), (0,)), ((), ()))
+    width = pin.shape[2]
+    chunk = 512
+
+    def gather(c, carry):
+        cols = pl.ds(pl.multiple_of(c * chunk, chunk), chunk)
+        rows = pin[:, :, cols].astype(jnp.float32).reshape(count, chunk)
+        out = lax.dot_general(place, rows, contract, preferred_element_type=jnp.float32)
+        fwd[:, :, cols] = out.reshape(local_n, FWD, chunk).astype(jnp.bfloat16)
+        return carry
+
+    lax.fori_loop(0, width // chunk, gather, 0)
+    fwd_meta[...] = lax.dot_general(
+        place, marks, contract, preferred_element_type=jnp.float32
+    ).reshape(local_n, FWD, 128)
+
+    def fwd_copies(k):
+        a, b = split(k)
+        tg, tu = lax.rem(g + a, n_grp), lax.rem(u + b, hd)
+        t = tg * hd + tu
+        to = (tg, half * hd + tu)
+        return [
+            remote(fwd.at[t], rows_out.at[fwd_base + me_local],
+                   fwd_sems.at[0, k], fwd_sems.at[1, k], to),
+            remote(fwd_meta.at[t], fmeta_out.at[me_local],
+                   fwdm_sems.at[0, k], fwdm_sems.at[1, k], to),
+        ]
+
+    own_fwd = [
+        local_copy(fwd.at[me_local], rows_out.at[fwd_base + me_local], 2),
+        local_copy(fwd_meta.at[me_local], fmeta_out.at[me_local], 3),
+    ]
+    for cp in own_fwd:
+        cp.start()
+
+    def send_fwd(k, c):
+        for cp in fwd_copies(k):
+            cp.start()
+        return c
+
+    lax.fori_loop(1, local_n, send_fwd, 0)
+    lax.fori_loop(1, local_n, send_near, 0)
+
+    for cp in piece_copies:
+        cp.wait_send()
+
+    def finish_far(k, c):
+        cp = far_copy(k)
+        cp.wait_send()
+        cp.wait_recv()
+        return c
+
+    def finish_near(k, c):
+        for cp in [near_copy(k)] + fwd_copies(k):
+            cp.wait_send()
+            cp.wait_recv()
+        return c
+
+    def finish_fm(k, c):
+        cp = fm_copy(lax.rem(me + k, n), me, k)
+        cp.wait_send()
+        cp.wait_recv()
+        return c
+
+    lax.fori_loop(1, n, finish_fm, 0)
+    lax.fori_loop(0, local_n, finish_far, 0)
+    lax.fori_loop(1, local_n, finish_near, 0)
+    for cp in own + own_fwd:
+        cp.wait()
+
+
+def relay_exchange(fm, slots, pmeta, n_grp, n_dev):
+    n = n_grp * n_dev
+    local_n = n // 2
+    width = slots.shape[2]
+    pieces = n_grp + 1
+    groups = local_n * (NEAR + FAR + FWD) // GROUP
+    anyspec = pl.BlockSpec(memory_space=pl.ANY)
+    sem = pltpu.SemaphoreType.DMA
+    return pl.pallas_call(
+        functools.partial(relay_kernel, n_grp, n_dev),
+        out_shape=(
+            jax.ShapeDtypeStruct(fm.shape, fm.dtype),
+            jax.ShapeDtypeStruct((groups, GROUP, width), slots.dtype),
+            jax.ShapeDtypeStruct((local_n, FWD, 128), jnp.float32),
+        ),
+        in_specs=[anyspec, anyspec, anyspec],
+        out_specs=(anyspec, anyspec, anyspec),
+        scratch_shapes=[
+            pltpu.VMEM((pieces, GROUP, width), slots.dtype),
+            pltpu.VMEM((pieces, GROUP, 128), jnp.float32),
+            pltpu.VMEM((local_n, FWD, width), slots.dtype),
+            pltpu.VMEM((local_n, FWD, 128), jnp.float32),
+            sem((2, n)),
+            sem((2, local_n)),
+            sem((2, local_n)),
+            sem((2, pieces)),
+            sem((2, pieces)),
+            sem((2, local_n)),
+            sem((2, local_n)),
+            sem((4,)),
+        ],
         compiler_params=pltpu.CompilerParams(collective_id=0, has_side_effects=True),
-    )(meta, rows)
-
-
-def local(
-    token_ids,
-    sensitivity,
-    last_hidden,
-    lengths,
-    norm_gain,
-    reward_head,
-    chosen_index,
-    rejected_index,
-    shard_owner,
-):
+    )(fm, slots, pmeta)
+
+
+def local(token_ids, sensitivity, last_hidden, lengths, norm_gain, reward_head,
+          chosen_index, rejected_index, shard_owner):
+    args = (token_ids, sensitivity, last_hidden, lengths, norm_gain, reward_head,
+            chosen_index, rejected_index, shard_owner)
+    resp_local, block_len = token_ids.shape
+    devices = shard_owner.shape[0]
+    n_grp, n_dev = lax.axis_size("grp"), lax.axis_size("dev")
+    capacity = max(2, (2 * resp_local * block_len + devices - 1) // devices)
+    if (capacity == NEAR and n_dev % 4 == 0 and devices * resp_local <= 128
+            and resp_local <= 4 and devices // 2 * FWD <= 128
+            and VOCAB // devices < 64 * 250):
+        return relay_local(*args)
+    prep = prepare(*args)
+    return plain_finish(prep, n_dev)
+
+
+def prepare(token_ids, sensitivity, last_hidden, lengths, norm_gain, reward_head,
+            chosen_index, rejected_index, shard_owner):
     resp_local, block_len = token_ids.shape
     width = sensitivity.shape[2]
     tok_local = resp_local * block_len
-    n_dev = lax.axis_size("dev")
     devices = shard_owner.shape[0]
-    responses = devices * resp_local
     shard_rows = VOCAB // devices
     capacity = max(2, (2 * tok_local + devices - 1) // devices)
-    cols = width // devices
-    lanes = -(-max(cols, capacity, resp_local) // 128) * 128
     hidden = last_hidden.astype(jnp.float32)
     normed = (
         hidden / jnp.sqrt(jnp.mean(hidden * hidden, axis=-1, keepdims=True) + 1e-05) * norm_gain
@@ -121,33 +375,67 @@
     offset = ids - shard_of * shard_rows
     shard_hot = shard_of[:, None] == jnp.arange(devices, dtype=jnp.int32)[None, :]
     owner = jnp.sum(jnp.where(shard_hot, shard_owner[None, :], 0), axis=1)
-    live_hot = (shard_hot & live[:, None]).astype(jnp.bfloat16)
+    owner_hot = (owner[:, None] == jnp.arange(devices, dtype=jnp.int32)[None, :]) & live[:, None]
+    live_hot = owner_hot.astype(jnp.bfloat16)
     token_pos = jnp.arange(tok_local, dtype=jnp.int32)
     earlier = (token_pos[:, None] > token_pos[None, :]).astype(jnp.bfloat16)
     before = jnp.dot(earlier, live_hot, preferred_element_type=jnp.float32)
     rank = jnp.sum(before * live_hot.astype(jnp.float32), axis=1).astype(jnp.int32)
-    slot = jnp.where(live, owner * capacity + rank, -1)
+    counts = jnp.sum(owner_hot.astype(jnp.int32), axis=0)
+    return dict(
+        sens=sensitivity.reshape(tok_local, width), normed=normed, own_reward=own_reward,
+        live=live, offset=offset, owner=owner, rank=rank, counts=counts,
+        owner_hot=owner_hot, resp=token_pos // block_len, capacity=capacity,
+        chosen_index=chosen_index, rejected_index=rejected_index, devices=devices,
+        shard_rows=shard_rows, resp_local=resp_local, width=width, tok_local=tok_local,
+    )
+
+
+def lane_pad(a, lanes):
+    return jnp.pad(a, ((0, 0), (0, lanes - a.shape[1])))[:, None, :]
+
+
+def reward_grads(p, reward):
+    responses = p["devices"] * p["resp_local"]
+    all_resp = jnp.arange(responses, dtype=jnp.int32)
+    sign_table = (p["chosen_index"][:, None] == all_resp[None, :]).astype(jnp.float32) - (
+        p["rejected_index"][:, None] == all_resp[None, :]
+    ).astype(jnp.float32)
+    margin = jnp.sum(sign_table * reward[None, :], axis=1)
+    push = -jax.nn.sigmoid(-margin)
+    return jnp.sum(sign_table * push[:, None], axis=0)
+
+
+def place_all(shard_rows, rows, targets, scale):
+    scaled = (scale[:, None] * rows).astype(jnp.bfloat16)
+    placing = (targets[None, :] == jnp.arange(shard_rows, dtype=jnp.int32)[:, None]).astype(
+        jnp.bfloat16
+    )
+    return jnp.dot(placing, scaled, preferred_element_type=jnp.float32).astype(jnp.bfloat16)
+
+
+def plain_finish(p, n_dev):
+    devices, capacity, resp_local = p["devices"], p["capacity"], p["resp_local"]
+    width = p["width"]
+    cols = width // devices
+    responses = devices * resp_local
+    lanes = -(-max(cols, capacity, resp_local) // 128) * 128
+    slot = jnp.where(p["live"], p["owner"] * capacity + p["rank"], -1)
     slot_match = slot[None, :] == jnp.arange(devices * capacity, dtype=jnp.int32)[:, None]
     outgoing = jnp.dot(
-        slot_match.astype(jnp.bfloat16),
-        sensitivity.reshape(tok_local, width),
-        preferred_element_type=jnp.float32,
+        slot_match.astype(jnp.bfloat16), p["sens"], preferred_element_type=jnp.float32
     ).astype(jnp.bfloat16)
-    code = (offset + 1) * resp_local + token_pos // block_len
+    code = (p["offset"] + 1) * resp_local + p["resp"]
     codes = jnp.sum(jnp.where(slot_match, code[None, :], 0), axis=1)
     codes = codes.reshape(devices, capacity)
     target_out = codes // resp_local - 1
     resp_out = codes - codes // resp_local * resp_local
-
-    def lane_pad(a):
-        return jnp.pad(a, ((0, 0), (0, lanes - a.shape[1])))[:, None, :]
-
-    normed_blocks = normed.reshape(resp_local, devices, cols).transpose(1, 0, 2)
+    normed_blocks = p["normed"].reshape(resp_local, devices, cols).transpose(1, 0, 2)
     meta = jnp.concatenate(
         [
-            lane_pad(target_out.astype(jnp.float32)),
-            lane_pad(resp_out.astype(jnp.float32)),
-            lane_pad(jnp.broadcast_to(own_reward[None, :], (devices, resp_local))),
+            lane_pad(target_out.astype(jnp.float32), lanes),
+            lane_pad(resp_out.astype(jnp.float32), lanes),
+            lane_pad(jnp.broadcast_to(p["own_reward"][None, :], (devices, resp_local)), lanes),
             jnp.zeros((devices, 1, lanes), jnp.float32),
             jnp.pad(normed_blocks, ((0, 0), (0, 0), (0, lanes - cols))),
         ],
@@ -158,38 +446,154 @@
     meta_in, arrived = exchange(
         meta, outgoing.reshape(devices, capacity, width), devices, n_dev
     )
-
     targets = meta_in[:, 0, :capacity].astype(jnp.int32).reshape(devices * capacity)
     resp_in = meta_in[:, 1, :capacity].astype(jnp.int32)
     reward = meta_in[:, 2, :resp_local].reshape(responses)
     normed_in = meta_in[:, 4 : 4 + resp_local, :cols]
-    all_resp = jnp.arange(responses, dtype=jnp.int32)
-    sign_table = (chosen_index[:, None] == all_resp[None, :]).astype(jnp.float32) - (
-        rejected_index[:, None] == all_resp[None, :]
-    ).astype(jnp.float32)
-    margin = jnp.sum(sign_table * reward[None, :], axis=1)
-    push = -jax.nn.sigmoid(-margin)
-    reward_grad = jnp.sum(sign_table * push[:, None], axis=0).reshape(devices, resp_local)
+    reward_grad = reward_grads(p, reward).reshape(devices, resp_local)
     head_grad = jnp.sum(reward_grad[:, :, None] * normed_in, axis=(0, 1))
     resp_hot = resp_in[:, :, None] == jnp.arange(resp_local, dtype=jnp.int32)[None, None, :]
     scale = jnp.sum(jnp.where(resp_hot, reward_grad[:, None, :], 0.0), axis=2)
     total = devices * capacity
-    scale = scale.reshape(total)
-    rows_in = arrived.reshape(total, width)
-
-    def place_all(operands):
+    owned = place_all(
+        p["shard_rows"], arrived.reshape(total, width), targets, scale.reshape(total)
+    )
+    return owned, head_grad
+
+
+def relay_local(*args):
+    n_grp, n_dev = lax.axis_size("grp"), lax.axis_size("dev")
+    p = prepare(*args)
+    devices, resp_local, width = p["devices"], p["resp_local"], p["width"]
+    hd = n_dev // 2
+    local_n = devices // 2
+    pieces = n_grp + 1
+    cols = width // devices
+    responses = devices * resp_local
+    g, v = lax.axis_index("grp"), lax.axis_index("dev")
+    half = v // hd
+    me = g * n_dev + v
+    owner, rank, live = p["owner"], p["rank"], p["live"]
+    owner_g, owner_v = owner // n_dev, owner % n_dev
+    owner_local = owner_g * hd + owner_v % hd
+    near = owner_v // hd == half
+    dev_ids = jnp.arange(devices, dtype=jnp.int32)
+    dev_far = dev_ids % n_dev // hd != half
+    over = jnp.where(dev_far, jnp.maximum(p["counts"] - FAR, 0), 0)
+    over_base = jnp.sum(jnp.where(dev_ids[None, :] < dev_ids[:, None], over[None, :], 0), axis=1)
+    j = jnp.sum(jnp.where(p["owner_hot"], over_base[None, :], 0), axis=1) + rank - FAR
+    far_start = local_n * NEAR
+    piece_start = far_start + local_n * FAR
+    slots = piece_start + pieces * GROUP
+    piece_slot = jnp.where(
+        j < pieces * GROUP, piece_start + j % pieces * GROUP + j // pieces, -1
+    )
+    slot = jnp.where(
+        near,
+        owner_local * NEAR + rank,
+        jnp.where(rank < FAR, far_start + owner_local * FAR + rank, piece_slot),
+    )
+    slot = jnp.where(live, slot, -1)
+    slot_match = slot[None, :] == jnp.arange(slots, dtype=jnp.int32)[:, None]
+    outgoing = jnp.dot(
+        slot_match.astype(jnp.bfloat16), p["sens"], preferred_element_type=jnp.float32
+    ).astype(jnp.bfloat16)
+    code = (p["offset"] + 1) * responses + me * resp_local + p["resp"]
+    shown = jnp.where(near | (rank < FAR), rank, -1)
+    direct = jnp.where(live & (shown >= 0), owner * NEAR + shown, -1)
+    direct_match = direct[None, :] == jnp.arange(devices * NEAR, dtype=jnp.int32)[:, None]
+    codes = jnp.sum(jnp.where(direct_match, code[None, :], 0), axis=1).reshape(devices, NEAR)
+    piece_match = slot_match[piece_start:]
+    piece_code = jnp.sum(jnp.where(piece_match, code[None, :], 0), axis=1)
+    piece_owner = jnp.sum(jnp.where(piece_match, owner_local[None, :], 0), axis=1)
+    piece_target = piece_code // responses
+    lane = jnp.arange(128, dtype=jnp.int32)[None, :]
+    pmeta = jnp.zeros((pieces * GROUP, 128), jnp.int32)
+    for i, col in enumerate(
+        (
+            (piece_code > 0).astype(jnp.int32),
+            piece_owner // hd,
+            piece_owner % hd,
+            piece_code % responses,
+            piece_target // 64,
+            piece_target % 64,
+        )
+    ):
+        pmeta = jnp.where(lane == i, col[:, None], pmeta)
+    pmeta = pmeta.astype(jnp.float32).reshape(pieces, GROUP, 128)
+    normed_blocks = p["normed"].reshape(resp_local, devices, cols).transpose(1, 0, 2)
+    fm = jnp.concatenate(
+        [
+            lane_pad(jnp.broadcast_to(p["own_reward"][None, :], (devices, resp_local)), 128),
+            lane_pad(codes.astype(jnp.float32), 128),
+            lane_pad(jnp.broadcast_to(over.astype(jnp.float32)[None, :], (devices, devices)), 128),
+            jnp.zeros((devices, 1, 128), jnp.float32),
+            jnp.pad(normed_blocks, ((0, 0), (0, 4 - resp_local), (0, 128 - cols))),
+        ],
+        axis=1,
+    )
+    fm_in, rows_in, fmeta_in = relay_exchange(
+        fm, outgoing.reshape(slots // GROUP, GROUP, width), pmeta, n_grp, n_dev
+    )
+
+    reward = fm_in[:, 0, :resp_local].reshape(responses)
+    reward_grad = reward_grads(p, reward)
+    normed_in = fm_in[:, 4 : 4 + resp_local, :cols]
+    head_grad = jnp.sum(
+        reward_grad.reshape(devices, resp_local)[:, :, None] * normed_in, axis=(0, 1)
+    )
+    all_codes = fm_in[:, 1, :NEAR].astype(jnp.int32).reshape(n_grp, 2, hd, NEAR)
+    near_codes = jnp.where(half == 0, all_codes[:, 0], all_codes[:, 1])
+    far_codes = jnp.where(half == 0, all_codes[:, 1], all_codes[:, 0])[..., :FAR]
+    fmeta = fmeta_in.astype(jnp.int32)
+    fwd_codes = (fmeta[..., 4] * 64 + fmeta[..., 5]) * responses + fmeta[..., 3]
+    in_codes = jnp.concatenate(
+        [near_codes.reshape(-1), far_codes.reshape(-1), fwd_codes.reshape(-1)]
+    )
+    targets = in_codes // responses - 1
+    resp_in = in_codes % responses
+    resp_hot = resp_in[:, None] == jnp.arange(responses, dtype=jnp.int32)[None, :]
+    scale = jnp.sum(jnp.where(resp_hot, reward_grad[None, :], 0.0), axis=1)
+
+    over_all = fm_in[:, 2, :devices].astype(jnp.int32)
+    same = dev_ids[:, None] < dev_ids[None, :]
+    base_all = jnp.sum(jnp.where(same[None], over_all[:, :, None], 0), axis=1)
+    src_g, src_u = dev_ids // n_dev, dev_ids % hd
+    here_g = jnp.arange(local_n, dtype=jnp.int32) // hd
+    here_u = jnp.arange(local_n, dtype=jnp.int32) % hd
+    load = jnp.zeros((local_n, devices), jnp.int32)
+    for q in range(pieces):
+        cnt = (base_all + over_all - q + pieces - 1) // pieces - (
+            base_all - q + pieces - 1
+        ) // pieces
+        if q < n_grp:
+            lands = ((src_g[None, :] + q) % n_grp == here_g[:, None]) & (
+                src_u[None, :] == here_u[:, None]
+            )
+        else:
+            lands = (src_g[None, :] == here_g[:, None]) & (
+                (src_u[None, :] + hd // 2) % hd == here_u[:, None]
+            )
+        load = load + jnp.sum(jnp.where(lands[:, :, None], cnt[None], 0), axis=1)
+    fits = (jnp.max(load) <= FWD) & (jnp.max(jnp.sum(over_all, axis=1)) <= pieces * GROUP)
+
+    total = rows_in.shape[0] * GROUP
+    rows = rows_in.reshape(total, width)
+
+    def relayed(operands):
         rows, targets, scale = operands
-        scaled = (scale[:, None] * rows).astype(jnp.bfloat16)
-        placing = (targets[None, :] == jnp.arange(shard_rows, dtype=jnp.int32)[:, None]).astype(
-            jnp.bfloat16
-        )
-        return jnp.dot(placing, scaled, preferred_element_type=jnp.float32).astype(jnp.bfloat16)
-
-    operands = (rows_in, targets, scale)
-    blocks, window = 3, total // 4
-    if shard_rows % (8 * blocks) or window % 128:
-        owned = place_all(operands)
-        return (owned, head_grad)
+        return place_rows(p["shard_rows"], rows, targets, scale)
+
+    def resend(operands):
+        return plain_finish(p, n_dev)[0]
+
+    owned = lax.cond(fits, relayed, resend, (rows, targets, scale))
+    return owned, head_grad
+
+
+def place_rows(shard_rows, rows, targets, scale):
+    total, width = rows.shape
+    blocks, window = 3, 256
     block_rows = shard_rows // blocks
     first_row = jnp.arange(blocks, dtype=jnp.int32) * block_rows
     in_block = (targets[:, None] >= first_row[None, :]) & (
@@ -203,7 +607,7 @@
     packed_slot = jnp.sum(jnp.where(in_block, rank_in + slot_base[None, :] + 1, 0), axis=1) - 1
     fits = jnp.max(jnp.sum(in_block.astype(jnp.int32), axis=0)) <= window
 
-    def place_packed(operands):
+    def packed_place(operands):
         rows, targets, scale = operands
         pack = packed_slot[None, :] == jnp.arange(blocks * window, dtype=jnp.int32)[:, None]
         packed_scale = jnp.sum(jnp.where(pack, scale[None, :], 0.0), axis=1)
@@ -220,8 +624,9 @@
         )
         return owned.astype(jnp.bfloat16).reshape(shard_rows, width)
 
-    owned = lax.cond(fits, place_packed, place_all, operands)
-    return (owned, head_grad)
+    return lax.cond(
+        fits, packed_place, lambda o: place_all(shard_rows, *o), (rows, targets, scale)
+    )
 
 
 def solution(mesh):

time: 252 us -> 215 us (0.85)
  Pallas kernels: 198 us -> 152 us
  other arithmetic: 10.8 us -> 16.9 us
    pallas_call x1, Pallas kernels: 198 us -> 152 us  [relay_exchange(): pl.pallas_call(functools.partial(relay_kernel, n_grp, n_dev), out_shape=(...]
    reduce_sum x11 -> x23, other arithmetic: 4.93 us -> 9.08 us  [the longest x1 1.57 us: relay_local(): jnp.sum(over_all, axis=1)]
where the time goes in v1:
time: 215 us; the launch traced here: 213 us
  Pallas kernels  152 us (71%)
  matrix products  37.5 us (17%)
  other arithmetic  16.9 us (8%)
  local copies, waits for them, and re-layouts  3.49 us (2%)
  between operations  2.24 us (1%)
    pallas_call x1, Pallas kernels, relay_exchange(): pl.pallas_call(functools.partial(relay_kernel, n_grp, n_dev), out_shape=(...  152 us
    dot_general x1, matrix products, packed_place(): lax.dot_general(placing.astype(jnp.bfloat16), packed.reshape(blocks, wind...  17.4 us
    dot_general x1, matrix products, packed_place(): jnp.dot(pack.astype(jnp.bfloat16), rows, preferred_element_type=jnp.float32)  11.7 us
    dot_general x1, matrix products, relay_local(): jnp.dot(slot_match.astype(jnp.bfloat16), p['sens'], preferred_element_typ...  7.72 us

profile of v1, /device:TPU:11, one launch (start us, length us, event | category | flops | bytes accessed | tf_op | source)
XLA Modules:
  0.0 213.5 jit_solution(17272234488613916205)
XLA Ops:
  0.6 0.7 fusion.69
  1.4 0.9 fusion.30
  2.4 0.7 lt.201
  3.2 0.7 broadcast_divide_fusion
  3.9 0.7 select_reduce_fusion.16
  5.3 0.7 select_select_fusion
  6.4 1.0 multiply_reduce_fusion.3
  7.5 0.8 concatenate.33.fm_ref
  8.9 0.7 select_convert_fusion.pmeta_ref
  9.6 7.7 %fusion.27.slots_ref = bf16[101,8,4096]{2,1,0:T(8,128)(2,1)} fusion(bf16[512,4096]{1,0:T(8,128)(2,1)} %bitcast.66, s32[512]{0:T(512)S(1)} %get-tuple-element.467), kind=kOutput, calls=%fused_computation.87 | convolution fusion | flops 3392720896 | bytes 10815488 | tf_op jit(solution)/shard_map/dot_general | solution.py:498
  17.4 152.4 %shard_map.104 = (f32[32,8,128]{2,1,0:T(8,128)}, bf16[112,8,4096]{2,1,0:T(8,128)(2,1)}, f32[16,8,128]{2,1,0:T(8,128)}) custom-call(f32[32,8,128]{2,1,0:T(8,128)} %concatenate.33.fm_ref, bf16[101,8,4096]{2,1,0:T(8,128)(2,1)} %fusion.27.slots_ref, f32[5,8,128]{2,1,0:T(8,128)} %select_convert_fusion.pmeta_ref), custom_call_target="tpu_custom_call" | custom-call | tf_op jit(solution)/shard_map/pallas_call | solution.py:314
  169.8 0.8 convert_element_type.219
  170.6 0.4 fusion.31
  171.2 1.6 fusion.79
  172.8 0.6 reduce_max.31
  174.1 0.9 slice_reduce_fusion.1
  175.6 1.5 multiply_reduce_fusion.2
  177.1 1.0 slice_convert_fusion.1
  179.6 0.6 add_reduce_fusion
  180.9 32.5 %conditional.2 = (bf16[4008,4096]{1,0:T(8,128)(2,1)}) conditional(s32[]{:T(128)} %convert_element_type.216, (s32[4,128]{1,0:T(4,128)S(1)}, s32[4,128]{1,0:T(4,128)S(1)}, s32[512]{0:T(512)S(1)}, s32[512]{0:T(512)S(1)}, s32[512]{0:T(512)S(1)}, /*index=5*/s32[512]{0:T(512)S(1)}, s32[512]{0:T(512)S(1)}, s32[512]{0:T(512)S(1)}, ...), branch_computations={%region_21.26_spmd, %region_26.35_spmd.clone} | conditional | flops 37956063232 | bytes 54258216 | solution.py:590
  181.4 0.6 reduce_max.32
  183.4 30.0 %conditional.3 = (bf16[4008,4096]{1,0:T(8,128)(2,1)}) conditional(s32[]{:T(128)} %convert_element_type.223, (s32[896]{0:T(1024)S(1)}, f32[896]{0:T(1024)S(1)}, bf16[896,4096]{1,0:T(8,128)(2,1)}) %tuple.97, (s32[1,3]{1,0:T(1,128)S(1)}, s32[896,3]{0,1:T(4,128)S(1)}, pred[896,3]{0,1:T(4,128)(4,1)S(1)}, s32[896]{0:T(1024)S(1)}, s32[3]{0:T(128)S(1)}, ...), branch_computations={%region_30.30_spmd, %region_31.34_spmd} | conditional | flops 29449867264 | bytes 52862480 | solution.py:627
  184.3 11.7 %multiply_convert_fusion.2 = bf16[768,4096]{1,0:T(8,128)(2,1)} fusion(bf16[896,4096]{1,0:T(8,128)(2,1)} %get-tuple-element.430, f32[768]{0:T(1024)S(1)} %select_reduce_fusion, s32[896]{0:T(1024)S(1)} %get-tuple-element.474), kind=kOutput, calls=%fused_computation.6 | convolution fusion | flops 5644124160 | bytes 13638144 | tf_op jit(solution)/shard_map/cond/branch_1_fun/cond/branch_1_fun/dot_general | solution.py:615
  196.0 17.4 %convolution_convert_fusion.1 = bf16[3,1336,4096]{2,1,0:T(8,128)(2,1)} fusion(bf16[3,256,4096]{2,1,0:T(8,128)(2,1)} %bitcast.50, s32[3,1336]{1,0:T(4,128)S(1)} %iota_add_fusion, s32[3,256]{1,0:T(4,128)S(1)} %sub.193), kind=kOutput, calls=%fused_computation.5 | convolution fusion | flops 8422828032 | bytes 39144096 | tf_op jit(solution)/shard_map/cond/branch_1_fun/cond/branch_1_fun/dot_general | solution.py:619
  (84 shorter events, 5.8 us)
Async XLA Ops:
  17.3 157.8 %copy-start.1 = (s32[64]{0:T(128)S(1)}, s32[64]{0:T(128)}, u32[]{:S(2)}) copy-start(s32[64]{0:T(128)} %param.19) | copy-start | bytes 772
  17.3 157.8 %copy-start.2 = (s32[64]{0:T(128)S(1)}, s32[64]{0:T(128)}, u32[]{:S(2)}) copy-start(s32[64]{0:T(128)} %param.20) | copy-start | bytes 772
  17.3 163.6 %copy-start = (s32[4,128]{1,0:T(4,128)S(1)}, s32[4,128]{1,0:T(4,128)}, u32[]{:S(2)}) copy-start(s32[4,128]{1,0:T(4,128)} %param.13) | copy-start | bytes 6148

commit v2 on v1

--- a/solution.py
+++ b/solution.py
@@ -215,7 +215,14 @@
         near_copy(k).start()
         return c
 
-    lax.fori_loop(0, local_n, send_far, 0)
+    far_copy(0).start()
+
+    def send_both(k, c):
+        far_copy(k).start()
+        near_copy(k).start()
+        return c
+
+    lax.fori_loop(1, 16, send_both, 0)
 
     for cp in piece_copies:
         cp.wait_recv()
@@ -273,7 +280,7 @@
         return c
 
     lax.fori_loop(1, local_n, send_fwd, 0)
-    lax.fori_loop(1, local_n, send_near, 0)
+    lax.fori_loop(16, local_n, send_both, 0)
 
     for cp in piece_copies:
         cp.wait_send()
@@ -591,42 +598,160 @@
     return owned, head_grad
 
 
+MAIN = 640
+CHUNK = 512
+BLOCK_ROWS = 512
+
+
+def place_kernel(count_ref, starts_ref, pos_ref, target_ref, scale_ref, rows_ref, out_ref,
+                 rows_v, sorted_v, pick, onehot, acc, outbuf, in_sems, out_sems):
+    total, width = rows_ref.shape
+    shard_rows = out_ref.shape[0]
+    chunks = width // CHUNK
+    blocks = -(-shard_rows // BLOCK_ROWS)
+
+    def fetch(c):
+        return pltpu.make_async_copy(
+            rows_ref.at[:, pl.ds(c * CHUNK, CHUNK)], rows_v.at[c], in_sems.at[c]
+        )
+
+    for c in range(chunks):
+        fetch(c).start()
+    rows_id = lax.broadcasted_iota(jnp.int32, (MAIN, total), 0)
+    pick[...] = jnp.where(rows_id == pos_ref[0:1, :], 1.0, 0.0).astype(jnp.bfloat16)
+    count = count_ref[0]
+    used = lax.max(lax.div(count + 127, 128), MAIN // 128)
+
+    for c in range(chunks):
+        fetch(c).wait()
+        got = jnp.dot(pick[...], rows_v[c], preferred_element_type=jnp.float32)
+        sorted_v[pl.ds(0, MAIN), pl.ds(c * CHUNK, CHUNK)] = (
+            scale_ref[pl.ds(0, MAIN), :] * got
+        ).astype(jnp.bfloat16)
+
+    def extra(m, carry):
+        base = pl.multiple_of(m * 128, 128)
+        ids = lax.broadcasted_iota(jnp.int32, (128, total), 0) + base
+        sel = jnp.where(ids == pos_ref[0:1, :], 1.0, 0.0).astype(jnp.bfloat16)
+        for c in range(chunks):
+            got = jnp.dot(sel, rows_v[c], preferred_element_type=jnp.float32)
+            sorted_v[pl.ds(base, 128), pl.ds(c * CHUNK, CHUNK)] = (
+                scale_ref[pl.ds(base, 128), :] * got
+            ).astype(jnp.bfloat16)
+        return carry
+
+    lax.fori_loop(MAIN // 128, used, extra, 0)
+    sorted_v[pl.ds(pl.multiple_of(used * 128, 128), 128), :] = jnp.zeros(
+        (128, width), jnp.bfloat16
+    )
+
+    def put(b):
+        size = min(BLOCK_ROWS, shard_rows - b * BLOCK_ROWS)
+        return pltpu.make_async_copy(
+            outbuf.at[b % 2, pl.ds(0, size)],
+            out_ref.at[pl.ds(b * BLOCK_ROWS, size)],
+            out_sems.at[b % 2],
+        )
+
+    for b in range(blocks):
+        size = min(BLOCK_ROWS, shard_rows - b * BLOCK_ROWS)
+        size16 = -(-size // 16) * 16
+        first, last = starts_ref[b], starts_ref[b + 1]
+        low = lax.div(first, 128) * 128
+        windows = lax.div(last - low + 255, 256)
+        if b >= 2:
+            put(b - 2).wait()
+        row_id = lax.broadcasted_iota(jnp.int32, (size16, 256), 0) + b * BLOCK_ROWS
+
+        def window(w):
+            at = pl.multiple_of(low + w * 256, 128)
+            return at, jnp.where(
+                row_id == target_ref[0:1, pl.ds(at, 256)], 1.0, 0.0
+            ).astype(jnp.bfloat16)
+
+        @pl.when(windows <= 1)
+        def _():
+            at, hot = window(0)
+            onehot[pl.ds(0, size16), :] = hot
+
+            def col(c, carry):
+                cols = pl.ds(pl.multiple_of(c * CHUNK, CHUNK), CHUNK)
+                outbuf[b % 2, pl.ds(0, size16), cols] = jnp.dot(
+                    onehot[pl.ds(0, size16), :],
+                    sorted_v[pl.ds(at, 256), cols],
+                    preferred_element_type=jnp.float32,
+                ).astype(jnp.bfloat16)
+                return carry
+
+            lax.fori_loop(0, chunks, col, 0)
+
+        @pl.when(windows > 1)
+        def _():
+            def col(c, carry):
+                cols = pl.ds(pl.multiple_of(c * CHUNK, CHUNK), CHUNK)
+                acc[...] = jnp.zeros_like(acc)
+
+                def add(w, carry):
+                    at, hot = window(w)
+                    acc[pl.ds(0, size16), :] += jnp.dot(
+                        hot, sorted_v[pl.ds(at, 256), cols],
+                        preferred_element_type=jnp.float32,
+                    )
+                    return carry
+
+                lax.fori_loop(0, windows, add, 0)
+                outbuf[b % 2, pl.ds(0, size16), cols] = acc[pl.ds(0, size16), :].astype(
+                    jnp.bfloat16
+                )
+                return carry
+
+            lax.fori_loop(0, chunks, col, 0)
+
+        put(b).start()
+    for b in range(max(0, blocks - 2), blocks):
+        put(b).wait()
+
+
 def place_rows(shard_rows, rows, targets, scale):
     total, width = rows.shape
-    blocks, window = 3, 256
-    block_rows = shard_rows // blocks
-    first_row = jnp.arange(blocks, dtype=jnp.int32) * block_rows
-    in_block = (targets[:, None] >= first_row[None, :]) & (
-        targets[:, None] < first_row[None, :] + block_rows
-    )
-    block_hot = in_block.astype(jnp.bfloat16)
-    pos = jnp.arange(total, dtype=jnp.int32)
-    ahead = (pos[:, None] > pos[None, :]).astype(jnp.bfloat16)
-    rank_in = jnp.dot(ahead, block_hot, preferred_element_type=jnp.float32).astype(jnp.int32)
-    slot_base = jnp.arange(blocks, dtype=jnp.int32) * window
-    packed_slot = jnp.sum(jnp.where(in_block, rank_in + slot_base[None, :] + 1, 0), axis=1) - 1
-    fits = jnp.max(jnp.sum(in_block.astype(jnp.int32), axis=0)) <= window
-
-    def packed_place(operands):
-        rows, targets, scale = operands
-        pack = packed_slot[None, :] == jnp.arange(blocks * window, dtype=jnp.int32)[:, None]
-        packed_scale = jnp.sum(jnp.where(pack, scale[None, :], 0.0), axis=1)
-        packed_target = jnp.sum(jnp.where(pack, targets[None, :] + 1, 0), axis=1) - 1
-        packed = jnp.dot(pack.astype(jnp.bfloat16), rows, preferred_element_type=jnp.float32)
-        packed = (packed_scale[:, None] * packed).astype(jnp.bfloat16)
-        row_of = first_row[:, None] + jnp.arange(block_rows, dtype=jnp.int32)[None, :]
-        placing = packed_target.reshape(blocks, 1, window) == row_of[:, :, None]
-        owned = lax.dot_general(
-            placing.astype(jnp.bfloat16),
-            packed.reshape(blocks, window, width),
-            (((2,), (1,)), ((0,), (0,))),
-            preferred_element_type=jnp.float32,
-        )
-        return owned.astype(jnp.bfloat16).reshape(shard_rows, width)
-
-    return lax.cond(
-        fits, packed_place, lambda o: place_all(shard_rows, *o), (rows, targets, scale)
-    )
+    cap = 1280
+    chunks = width // CHUNK
+    blocks = -(-shard_rows // BLOCK_ROWS)
+    index = jnp.arange(total, dtype=jnp.int32)
+    live = targets >= 0
+    key = jnp.where(live, targets * 2048 + index, 1 << 30)
+    pos = jnp.sum((key[:, None] < key[None, :]).astype(jnp.int32), axis=0)
+    pos = jnp.where(live, pos, -1)
+    place = jnp.arange(cap, dtype=jnp.int32)
+    hot = pos[:, None] == place[None, :]
+    sorted_target = jnp.sum(jnp.where(hot, targets[:, None] + 1, 0), axis=0) - 1
+    sorted_scale = jnp.sum(
+        jnp.where(pos[None, :] == place[:, None], scale[None, :], 0.0), axis=1
+    )
+    limit = jnp.arange(blocks + 1, dtype=jnp.int32) * BLOCK_ROWS
+    starts = jnp.sum(
+        (live[None, :] & (targets[None, :] < limit[:, None])).astype(jnp.int32), axis=1
+    )
+    smem = pl.BlockSpec(memory_space=pltpu.SMEM)
+    vmem = pl.BlockSpec(memory_space=pltpu.VMEM)
+    anyspec = pl.BlockSpec(memory_space=pl.ANY)
+    return pl.pallas_call(
+        place_kernel,
+        out_shape=jax.ShapeDtypeStruct((shard_rows, width), rows.dtype),
+        in_specs=[smem, smem, vmem, vmem, vmem, anyspec],
+        out_specs=anyspec,
+        scratch_shapes=[
+            pltpu.VMEM((chunks, total, CHUNK), jnp.bfloat16),
+            pltpu.VMEM((cap, width), jnp.bfloat16),
+            pltpu.VMEM((MAIN, total), jnp.bfloat16),
+            pltpu.VMEM((BLOCK_ROWS, 256), jnp.bfloat16),
+            pltpu.VMEM((BLOCK_ROWS, CHUNK), jnp.float32),
+            pltpu.VMEM((2, BLOCK_ROWS, width), jnp.bfloat16),
+            pltpu.SemaphoreType.DMA((chunks,)),
+            pltpu.SemaphoreType.DMA((2,)),
+        ],
+        compiler_params=pltpu.CompilerParams(vmem_limit_bytes=60 * 1024 * 1024),
+    )(starts[blocks:], starts, pos[None, :], sorted_target[None, :], sorted_scale[:, None], rows)
 
 
 def solution(mesh):

time: 215 us -> 191 us (0.89)
  matrix products: 37.5 us -> 8 us
  Pallas kernels: 152 us -> 156 us
  local copies, waits for them, and re-layouts: 3.49 us -> 6.34 us
    pallas_call x0 -> x1, Pallas kernels: none -> 31.3 us  [place_rows(): pl.pallas_call(place_kernel, out_shape=jax.ShapeDtypeStruct((shard_rows,...]
    dot_general x3 -> x0, matrix products: 29.5 us -> none  [the longest x1 17.4 us: packed_place(): lax.dot_general(placing.astype(jnp.bfloat16), packed.reshape(blocks, wind...]
    pallas_call x1, Pallas kernels: 152 us -> 125 us  [relay_exchange(): pl.pallas_call(functools.partial(relay_kernel, n_grp, n_dev), out_shape=(...]
where the time goes in v2:
time: 191 us; the launch traced here: 190 us
  Pallas kernels  156 us (82%)
  other arithmetic  17 us (9%)
  matrix products  8 us (4%)
  local copies, waits for them, and re-layouts  6.34 us (3%)
  between operations  2.4 us (1%)
    pallas_call x1, Pallas kernels, relay_exchange(): pl.pallas_call(functools.partial(relay_kernel, n_grp, n_dev), out_shape=(...  125 us
    pallas_call x1, Pallas kernels, place_rows(): pl.pallas_call(place_kernel, out_shape=jax.ShapeDtypeStruct((shard_rows,...  31.3 us
    dot_general x1, matrix products, relay_local(): jnp.dot(slot_match.astype(jnp.bfloat16), p['sens'], preferred_element_typ...  7.72 us

profile of v2, /device:TPU:11, one launch (start us, length us, event | category | flops | bytes accessed | tf_op | source)
XLA Modules:
  0.0 190.0 jit_solution(17056067814922536143)
XLA Ops:
  0.6 0.7 fusion.60
  1.4 0.9 fusion.21
  2.4 0.7 lt.228
  3.2 0.7 broadcast_divide_fusion
  3.9 0.7 select_reduce_fusion.15
  5.3 0.7 select_select_fusion
  6.4 1.0 multiply_reduce_fusion.3
  7.5 0.8 concatenate.33.fm_ref
  8.9 0.7 select_convert_fusion.pmeta_ref
  9.6 7.7 %fusion.18.slots_ref = bf16[101,8,4096]{2,1,0:T(8,128)(2,1)} fusion(bf16[512,4096]{1,0:T(8,128)(2,1)} %bitcast.57, s32[512]{0:T(512)S(1)} %get-tuple-element.382), kind=kOutput, calls=%fused_computation.70 | convolution fusion | flops 3392720896 | bytes 10815488 | tf_op jit(solution)/shard_map/dot_general | solution.py:505
  17.4 124.7 %shard_map.104 = (f32[32,8,128]{2,1,0:T(8,128)}, bf16[112,8,4096]{2,1,0:T(8,128)(2,1)}, f32[16,8,128]{2,1,0:T(8,128)}) custom-call(f32[32,8,128]{2,1,0:T(8,128)} %concatenate.33.fm_ref, bf16[101,8,4096]{2,1,0:T(8,128)(2,1)} %fusion.18.slots_ref, f32[5,8,128]{2,1,0:T(8,128)} %select_convert_fusion.pmeta_ref), custom_call_target="tpu_custom_call" | custom-call | tf_op jit(solution)/shard_map/pallas_call | solution.py:321
  142.1 0.8 convert_element_type.191
  143.6 1.6 fusion.70
  145.1 0.6 reduce_max.19
  146.4 0.9 slice_reduce_fusion.1
  147.9 1.5 multiply_reduce_fusion.2
  149.5 1.0 slice_convert_fusion.1
  152.0 0.6 add_reduce_fusion
  153.3 36.6 %conditional.1 = (bf16[4008,4096]{1,0:T(8,128)(2,1)}) conditional(s32[]{:T(128)} %convert_element_type.188, (s32[4,128]{1,0:T(4,128)S(1)}, s32[4,128]{1,0:T(4,128)S(1)}, s32[512]{0:T(512)S(1)}, s32[512]{0:T(512)S(1)}, s32[512]{0:T(512)S(1)}, /*index=5*/s32[512]{0:T(512)S(1)}, s32[512]{0:T(512)S(1)}, s32[512]{0:T(512)S(1)}, ...), branch_computations={%region_21.26_spmd, %region_26.32_spmd.clone} | conditional | flops 37956063232 | bytes 54258216 | solution.py:597
  154.5 0.6 slice.61.count_ref
  155.1 0.6 broadcast_in_dim.494.pos_ref
  156.2 0.6 select_reduce_fusion.1
  157.5 1.1 broadcast_in_dim.502.scale_ref
  158.5 31.3 %branch_1_fun.4 = bf16[4008,4096]{1,0:T(8,128)(2,1)} custom-call(s32[1]{0:T(128)} %slice.61.count_ref, s32[9]{0:T(128)} %copy-done.3, s32[1,896]{1,0:T(1,128)} %broadcast_in_dim.494.pos_ref, s32[1,1280]{1,0:T(1,128)} %sub.289.target_ref, f32[1280,1]{1,0:T(8,128)} %broadcast_in_dim.502.scale_ref, bf16[896,4096]{1,0:T(8,128)(2,1)} %bitcast.43), custom_call_target="tpu_custom_call" | custom-call | tf_op jit(solution)/shard_map/cond/branch_1_fun/pallas_call | solution.py:738
  (80 shorter events, 6.4 us)
Async XLA Ops:
  17.3 130.1 %copy-start.1 = (s32[64]{0:T(128)S(1)}, s32[64]{0:T(128)}, u32[]{:S(2)}) copy-start(s32[64]{0:T(128)} %param.17) | copy-start | bytes 772
  17.3 130.1 %copy-start.2 = (s32[64]{0:T(128)S(1)}, s32[64]{0:T(128)}, u32[]{:S(2)}) copy-start(s32[64]{0:T(128)} %param.18) | copy-start | bytes 772
  17.4 135.9 %copy-start = (s32[4,128]{1,0:T(4,128)S(1)}, s32[4,128]{1,0:T(4,128)}, u32[]{:S(2)}) copy-start(s32[4,128]{1,0:T(4,128)} %param.11) | copy-start | bytes 6148
  154.5 4.1 %copy-start.3 = (s32[9]{0:T(128)}, s32[9]{0:T(128)S(1)}, u32[]{:S(2)}) copy-start(s32[9]{0:T(128)S(1)} %convert_reduce_fusion.1.starts_ref) | copy-start | bytes 112 | tf_op jit(solution)/shard_map/cond

commit v3 on v1

v3 whole, which is shorter than its diff:
```python
import functools

import jax
import jax.numpy as jnp
from jax import lax
from jax.experimental import pallas as pl
from jax.experimental.pallas import tpu as pltpu
from jax.sharding import PartitionSpec as P

VOCAB = 128256
MESH = pl.DeviceIdType.MESH


def exchange_kernel(n, n_dev, meta_ref, rows_ref, meta_out, rows_out, send_sem, recv_sem, own_sem):
    me = lax.axis_index("grp") * n_dev + lax.axis_index("dev")

    def coord(t):
        return (t // n_dev, lax.rem(t, n_dev))

    barrier = pltpu.get_barrier_semaphore()

    def greet(k, c):
        t = lax.rem(me + k, n)
        pl.semaphore_signal(barrier, inc=1, device_id=coord(t), device_id_type=MESH)
        return c

    lax.fori_loop(1, n, greet, 0)
    own = [
        pltpu.make_async_copy(src.at[me], dst.at[me], own_sem.at[i])
        for i, (src, dst) in enumerate(((meta_ref, meta_out), (rows_ref, rows_out)))
    ]
    for c in own:
        c.start()
    pl.semaphore_wait(barrier, n - 1)

    def copies(src_block, dst_block, to):
        return [
            pltpu.make_async_remote_copy(
                src_ref=src.at[src_block],
                dst_ref=dst.at[dst_block],
                send_sem=send_sem.at[i, src_block],
                recv_sem=recv_sem.at[i, dst_block],
                device_id=coord(to),
                device_id_type=MESH,
            )
            for i, (src, dst) in enumerate(((meta_ref, meta_out), (rows_ref, rows_out)))
        ]

    def send(k, c):
        t = lax.rem(me + k, n)
        for cp in copies(t, me, t):
            cp.start()
        return c

    lax.fori_loop(1, n, send, 0)

    def finish(k, c):
        t = lax.rem(me + k, n)
        for cp in copies(t, me, t):
            cp.wait_send()
        s = lax.rem(me + n - k, n)
        for cp in copies(s, s, s):
            cp.wait_recv()
        return c

    lax.fori_loop(1, n, finish, 0)
    for c in own:
        c.wait()


def exchange(meta, rows, n, n_dev):
    anyspec = pl.BlockSpec(memory_space=pl.ANY)
    return pl.pallas_call(
        functools.partial(exchange_kernel, n, n_dev),
        out_shape=(
            jax.ShapeDtypeStruct(meta.shape, meta.dtype),
            jax.ShapeDtypeStruct(rows.shape, rows.dtype),
        ),
        in_specs=[anyspec, anyspec],
        out_specs=(anyspec, anyspec),
        scratch_shapes=[
            pltpu.SemaphoreType.DMA((2, n)),
            pltpu.SemaphoreType.DMA((2, n)),
            pltpu.SemaphoreType.DMA((2,)),
        ],
        compiler_params=pltpu.CompilerParams(collective_id=1, has_side_effects=True),
    )(meta, rows)


GROUP = 8
NEAR = 32
FAR = 16
FWD = 8
WINDOW = 256
BLOCKS = 3
CHUNK = 512
EARLY = 8
LATE = 12


def near_row(k):
    return k * NEAR + (k // EARLY) * 128 + (k // LATE) * 128


def far_row(k):
    return 256 + k * FAR + (k // EARLY) * 128


def relay_kernel(n_grp, n_dev, block_rows, fm_ref, slots_ref, pmeta_ref, chosen_ref,
                 rejected_ref, rows_out, packed_out, where_out, slot_out, head_out, flag_out,
                 rin, fin, fm_in, pin, pmeta_in, fwd, fwd_meta, fmeta_in, picks, scales, packed,
                 fm_sems, near_sems, far_sems, piece_sems, pm_sems, fwd_sems, fwdm_sems,
                 own_sems, save_sems, pack_sems):
    g = lax.axis_index("grp")
    v = lax.axis_index("dev")
    hd = n_dev // 2
    local_n = n_grp * hd
    half = v // hd
    u = lax.rem(v, hd)
    me = g * n_dev + v
    n = n_grp * n_dev
    pieces = n_grp + 1
    direct = local_n * (NEAR + FAR)
    far_base = local_n * NEAR
    other = 1 - half
    width = slots_ref.shape[1]
    f32 = jnp.float32

    def coord(t):
        return (t // n_dev, lax.rem(t, n_dev))

    barrier = pltpu.get_barrier_semaphore()

    def greet(k, c):
        pl.semaphore_signal(
            barrier, inc=1, device_id=coord(lax.rem(me + k, n)), device_id_type=MESH
        )
        return c

    lax.fori_loop(1, n, greet, 0)
    own = [
        pltpu.make_async_copy(fm_ref.at[me], fm_in.at[0], own_sems.at[0]),
        pltpu.make_async_copy(
            slots_ref.at[pl.ds(0, NEAR)], rin.at[pl.ds(0, NEAR)], own_sems.at[1]
        ),
    ]
    for cp in own:
        cp.start()
    pl.semaphore_wait(barrier, n - 1)

    def remote(src, dst, send_sem, recv_sem, to):
        return pltpu.make_async_remote_copy(
            src_ref=src, dst_ref=dst, send_sem=send_sem, recv_sem=recv_sem,
            device_id=to, device_id_type=MESH,
        )

    def partner(k, side):
        return lax.rem(g + k // hd, n_grp), side * hd + lax.rem(u + lax.rem(k, hd), hd)

    def piece_target(q):
        if q < n_grp:
            return (lax.rem(g + q, n_grp), other * hd + u)
        return (g, other * hd + lax.rem(u + hd // 2, hd))

    piece_copies = []
    for q in range(pieces):
        to = piece_target(q)
        piece_copies.append(
            remote(slots_ref.at[pl.ds(direct + q * GROUP, GROUP)], pin.at[q],
                   piece_sems.at[0, q], piece_sems.at[1, q], to)
        )
        piece_copies.append(
            remote(pmeta_ref.at[q], pmeta_in.at[q], pm_sems.at[0, q], pm_sems.at[1, q], to)
        )
    for cp in piece_copies:
        cp.start()

    def fm_copy(r):
        side = lax.rem(half + r // local_n, 2)
        tg, tv = partner(lax.rem(r, local_n), side)
        return remote(fm_ref.at[tg * n_dev + tv], fm_in.at[r], fm_sems.at[0, r],
                      fm_sems.at[1, r], (tg, tv))

    def near_copy(k):
        return remote(
            slots_ref.at[pl.ds(k * NEAR, NEAR)], rin.at[pl.ds(near_row(k), NEAR)],
            near_sems.at[0, k], near_sems.at[1, k], partner(k, half),
        )

    def far_copy(k):
        return remote(
            slots_ref.at[pl.ds(far_base + k * FAR, FAR)], rin.at[pl.ds(far_row(k), FAR)],
            far_sems.at[0, k], far_sems.at[1, k], partner(k, other),
        )

    def fwd_copies(k):
        to = partner(k, half)
        return [
            remote(fwd.at[k], fin.at[k], fwd_sems.at[0, k], fwd_sems.at[1, k], to),
            remote(fwd_meta.at[k], fmeta_in.at[k], fwdm_sems.at[0, k], fwdm_sems.at[1, k], to),
        ]

    def send_fm(r, c):
        fm_copy(r).start()
        return c

    lax.fori_loop(1, n, send_fm, 0)
    far_copy(0).start()

    def send_both(k, c):
        far_copy(k).start()
        near_copy(k).start()
        return c

    lax.fori_loop(1, local_n, send_both, 0)

    for cp in piece_copies:
        cp.wait_recv()
    count = pieces * GROUP
    marks = pmeta_in[...].reshape(count, 128)
    used = marks[:, 0:1] > 0.0
    dst_g = marks[:, 1:2].astype(jnp.int32)
    dst_u = marks[:, 2:3].astype(jnp.int32)
    dst = ((dst_g - g) & (n_grp - 1)) * hd + ((dst_u - u) & (hd - 1))
    lane = lax.broadcasted_iota(jnp.int32, (count, 128), 1)
    hot = jnp.where((lane == dst) & used, 1.0, 0.0)
    row_i = lax.broadcasted_iota(jnp.int32, (count, count), 0)
    col_i = lax.broadcasted_iota(jnp.int32, (count, count), 1)
    earlier = jnp.where(row_i > col_i, 1.0, 0.0)
    before = jnp.dot(earlier, hot, preferred_element_type=f32)
    rank = jnp.sum(before * hot, axis=1, keepdims=True).astype(jnp.int32)
    slot = jnp.where(used & (rank < FWD), dst * FWD + rank, -1)
    place = jnp.where(lane == slot, 1.0, 0.0)
    contract = (((0,), (0,)), ((), ()))
    rows_rows = (((1,), (1,)), ((), ()))

    def gather(c, carry):
        cols = pl.ds(pl.multiple_of(c * CHUNK, CHUNK), CHUNK)
        rows = pin[:, :, cols].astype(f32).reshape(count, CHUNK)
        out = lax.dot_general(place, rows, contract, preferred_element_type=f32)
        out = out.reshape(local_n, FWD, CHUNK).astype(jnp.bfloat16)
        fwd[:, :, cols] = out
        fin[0, :, cols] = out[0]
        return carry

    lax.fori_loop(0, width // CHUNK, gather, 0)
    out_meta = lax.dot_general(place, marks, contract, preferred_element_type=f32)
    out_meta = out_meta.reshape(local_n, FWD, 128)
    fwd_meta[...] = out_meta
    fmeta_in[0] = out_meta[0]

    def send_fwd(k, c):
        for cp in fwd_copies(k):
            cp.start()
        return c

    lax.fori_loop(1, local_n, send_fwd, 0)

    def wait_fm(r, c):
        cp = fm_copy(r)
        cp.wait_send()
        cp.wait_recv()
        return c

    own[0].wait()
    lax.fori_loop(1, n, wait_fm, 0)

    def source(r):
        a, b = (r & (local_n - 1)) // hd, r & (hd - 1)
        side = (half - r // local_n) & 1
        sg, su = (g - a) & (n_grp - 1), (u - b) & (hd - 1)
        return sg, su, sg * n_dev + side * hd + su

    reward = jnp.sum(fm_in[:, 0, :], axis=0, keepdims=True)
    pairs = chosen_ref.shape[0]
    pair_lane = lax.broadcasted_iota(jnp.int32, (pairs, 128), 1)
    sign = jnp.where(chosen_ref[...] == pair_lane, 1.0, 0.0) - jnp.where(
        rejected_ref[...] == pair_lane, 1.0, 0.0
    )
    margin = jnp.sum(sign * reward, axis=1, keepdims=True)
    push = -1.0 / (1.0 + jnp.exp(margin))
    reward_grad = jnp.sum(sign * push, axis=0, keepdims=True)
    eye0 = lax.broadcasted_iota(jnp.int32, (128, 128), 0)
    eye1 = lax.broadcasted_iota(jnp.int32, (128, 128), 1)
    grad_col = jnp.sum(jnp.where(eye0 == eye1, reward_grad, 0.0), axis=1, keepdims=True)
    src_lane = lax.broadcasted_iota(jnp.int32, (n, 128), 1)
    _, _, src = source(lax.broadcasted_iota(jnp.int32, (n, 128), 0))
    head = jnp.zeros((1, 128), f32)
    for j in range(4):
        part = jnp.where(src_lane == src * 4 + j, reward_grad, 0.0)
        coef = jnp.sum(part, axis=1, keepdims=True)
        head = head + jnp.sum(coef * fm_in[:, 4 + j, :], axis=0, keepdims=True)
    head_out[...] = jnp.broadcast_to(head, (8, 128))

    over = fm_in[:, 2, :]
    upper = jnp.where(eye0 < eye1, 1.0, 0.0)
    over_base = jnp.dot(over, upper, preferred_element_type=f32)
    here = lax.broadcasted_iota(jnp.int32, (local_n, n), 0)
    from_g, from_u, _ = source(lax.broadcasted_iota(jnp.int32, (local_n, n), 1))
    load = jnp.zeros((local_n, 128), f32)
    for q in range(pieces):
        part = jnp.floor((over_base + over - q + pieces - 0.5) * (1.0 / pieces)) - jnp.floor(
            (over_base - q + pieces - 0.5) * (1.0 / pieces)
        )
        if q < n_grp:
            at = ((from_g + q) & (n_grp - 1)) * hd + from_u
        else:
            at = from_g * hd + ((from_u + hd // 2) & (hd - 1))
        lands = jnp.where(at == here, 1.0, 0.0)
        load = load + jnp.dot(lands, part, preferred_element_type=f32)
    excess = jnp.maximum(
        jnp.max(jnp.max(load, axis=1, keepdims=True), axis=0, keepdims=True) - FWD,
        jnp.max(jnp.sum(over, axis=1, keepdims=True), axis=0, keepdims=True) - count,
    )

    def code_row(start, size):
        return jnp.sum(fm_in[pl.ds(start, size), 1, :], axis=0, keepdims=True)

    code_rows = [
        code_row(0, 4), code_row(4, 4), code_row(local_n, 8),
        code_row(8, 4), code_row(local_n + 8, 8), code_row(12, 4),
    ]
    tri = jnp.where(eye0 < eye1, 1.0, 0.0)
    sub = lax.broadcasted_iota(jnp.int32, (8, 128), 0)
    resp_id = eye0
    total = packed.shape[0]
    packed_id = lax.broadcasted_iota(jnp.int32, (total, 128), 0)

    def index_tile(i, target, resp, filled, worst, found):
        begin = sub * block_rows
        inside = (target >= begin) & (target < begin + block_rows) & (target >= 0)
        hot_b = jnp.where(inside, 1.0, 0.0)
        ahead = jnp.dot(hot_b, tri, preferred_element_type=f32) + filled
        rank_b = jnp.sum(hot_b * ahead, axis=0, keepdims=True).astype(jnp.int32)
        block = jnp.sum(jnp.where(inside, sub, 0), axis=0, keepdims=True)
        live = target >= 0
        ok = live & (rank_b < WINDOW)
        pos = jnp.where(ok, block * WINDOW + rank_b, -1)
        pick = jnp.where(packed_id == pos, 1.0, 0.0)
        picks[i] = pick.astype(jnp.bfloat16)
        scale = jnp.sum(jnp.where(resp_id == resp, grad_col, 0.0), axis=0, keepdims=True)
        scale = jnp.where(live, scale, 0.0)
        got = jnp.sum(pick * scale, axis=1, keepdims=True)
        marked = jnp.where(live, target + 1, 0)
        digits = jnp.where(sub == 0, marked >> 6, jnp.where(sub == 1, marked & 63, 0))
        found = found + lax.dot_general(
            digits.astype(f32), pick, rows_rows, preferred_element_type=f32
        )
        slot_out[i, 0:1, :] = (marked - 1).astype(f32)
        slot_out[i, 1:2, :] = scale
        filled = filled + jnp.sum(hot_b, axis=1, keepdims=True)
        worst = jnp.maximum(worst, jnp.max(filled, axis=0, keepdims=True))
        return filled, worst, found, got

    slot_out[...] = jnp.zeros_like(slot_out)
    filled = jnp.zeros((8, 1), f32)
    worst = jnp.zeros((1, 1), f32)
    found = jnp.zeros((8, total), f32)
    for i, row in enumerate(code_rows):
        code = row.astype(jnp.int32)
        filled, worst, found, got = index_tile(
            i, (code >> 7) - 1, code & 127, filled, worst, found
        )
        if i % 2 == 0:
            scales[i // 2] = got
        else:
            scales[i // 2] = scales[i // 2] + got

    def pack(seg, first):
        def col(c, carry):
            cols = pl.ds(pl.multiple_of(c * CHUNK, CHUNK), CHUNK)
            got = jnp.dot(picks[2 * seg], rin[pl.ds(seg * 256, 128), cols],
                          preferred_element_type=f32)
            got = got + jnp.dot(picks[2 * seg + 1], rin[pl.ds(seg * 256 + 128, 128), cols],
                                preferred_element_type=f32)
            got = (scales[seg] * got).astype(jnp.bfloat16)
            packed[:, cols] = got if first else packed[:, cols] + got
            return carry

        lax.fori_loop(0, width // CHUNK, col, 0)

    def save(i, src, start, size):
        return pltpu.make_async_copy(src, rows_out.at[pl.ds(start, size)], save_sems.at[i])

    def wait_far(k, c):
        cp = far_copy(k)
        cp.wait_send()
        cp.wait_recv()
        return c

    def wait_near(k, c):
        cp = near_copy(k)
        cp.wait_send()
        cp.wait_recv()
        return c

    own[1].wait()
    saves = [save(i, rin.at[pl.ds(i * 256, 256)], i * 256, 256) for i in range(3)]
    lax.fori_loop(1, EARLY, wait_near, 0)
    saves[0].start()
    pack(0, True)
    lax.fori_loop(0, EARLY, wait_far, 0)
    lax.fori_loop(EARLY, LATE, wait_near, 0)
    saves[1].start()
    pack(1, False)
    for cp in piece_copies:
        cp.wait_send()
    lax.fori_loop(EARLY, local_n, wait_far, 0)
    lax.fori_loop(LATE, local_n, wait_near, 0)
    saves[2].start()
    pack(2, False)

    def wait_fwd(k, c):
        for cp in fwd_copies(k):
            cp.wait_send()
            cp.wait_recv()
        return c

    lax.fori_loop(1, local_n, wait_fwd, 0)
    fmeta = fmeta_in[...].reshape(128, 128)
    pick_rows = jnp.where(
        lax.broadcasted_iota(jnp.int32, (8, 128), 0)
        == lax.broadcasted_iota(jnp.int32, (8, 128), 1), 1.0, 0.0
    )
    meta_rows = lax.dot_general(pick_rows, fmeta, rows_rows, preferred_element_type=f32)
    meta_rows = meta_rows.astype(jnp.int32)
    target = meta_rows[4:5] * 64 + meta_rows[5:6] - 1
    filled, worst, found, got = index_tile(6, target, meta_rows[3:4], filled, worst, found)
    scales[3] = got

    def pack_out(c):
        cols = pl.ds(c * CHUNK, CHUNK)
        return pltpu.make_async_copy(packed.at[:, cols], packed_out.at[:, cols], pack_sems.at[c])

    for c in range(width // CHUNK):
        cols = pl.ds(c * CHUNK, CHUNK)
        rows = fin[:, :, cols].astype(f32).reshape(128, CHUNK)
        got = jnp.dot(picks[6].astype(f32), rows, preferred_element_type=f32)
        packed[:, cols] = packed[:, cols] + (scales[3] * got).astype(jnp.bfloat16)
        pack_out(c).start()
    fwd_save = []
    for k in range(local_n):
        fwd_save.append(save(3 + k, fin.at[k], direct + k * FWD, FWD))
        fwd_save[-1].start()
    where_out[...] = found[0:1] * 64.0 + found[1:2] - 1.0 + jnp.zeros((8, total), f32)
    flag_out[0:1, :] = jnp.broadcast_to(excess, (1, 128))
    flag_out[1:8, :] = jnp.broadcast_to(worst - WINDOW, (7, 128))
    for cp in saves + fwd_save:
        cp.wait()
    for c in range(width // CHUNK):
        pack_out(c).wait()


def relay_exchange(fm, slots, pmeta, chosen, rejected, n_grp, n_dev, block_rows):
    n = n_grp * n_dev
    local_n = n // 2
    width = slots.shape[1]
    pieces = n_grp + 1
    direct = local_n * (NEAR + FAR)
    rows = direct + local_n * FWD
    total = BLOCKS * WINDOW
    anyspec = pl.BlockSpec(memory_space=pl.ANY)
    vmem = pl.BlockSpec(memory_space=pltpu.VMEM)
    sem = pltpu.SemaphoreType.DMA
    bf16, f32 = jnp.bfloat16, jnp.float32
    return pl.pallas_call(
        functools.partial(relay_kernel, n_grp, n_dev, block_rows),
        out_shape=(
            jax.ShapeDtypeStruct((rows, width), bf16),
            jax.ShapeDtypeStruct((total, width), bf16),
            jax.ShapeDtypeStruct((8, total), f32),
            jax.ShapeDtypeStruct((rows // 128, 8, 128), f32),
            jax.ShapeDtypeStruct((8, 128), f32),
            jax.ShapeDtypeStruct((8, 128), f32),
        ),
        in_specs=[anyspec, anyspec, anyspec, vmem, vmem],
        out_specs=(anyspec, anyspec, vmem, vmem, vmem, vmem),
        scratch_shapes=[
            pltpu.VMEM((direct, width), bf16),
            pltpu.VMEM((local_n, FWD, width), bf16),
            pltpu.VMEM((n, 8, 128), f32),
            pltpu.VMEM((pieces, GROUP, width), bf16),
            pltpu.VMEM((pieces, GROUP, 128), f32),
            pltpu.VMEM((local_n, FWD, width), bf16),
            pltpu.VMEM((local_n, FWD, 128), f32),
            pltpu.VMEM((local_n, FWD, 128), f32),
            pltpu.VMEM((rows // 128, total, 128), bf16),
            pltpu.VMEM((4, total, 1), f32),
            pltpu.VMEM((total, width), bf16),
            sem((2, n)),
            sem((2, local_n)),
            sem((2, local_n)),
            sem((2, pieces)),
            sem((2, pieces)),
            sem((2, local_n)),
            sem((2, local_n)),
            sem((2,)),
            sem((3 + local_n,)),
            sem((width // CHUNK,)),
        ],
        compiler_params=pltpu.CompilerParams(
            collective_id=0, has_side_effects=True, vmem_limit_bytes=56 * 1024 * 1024
        ),
    )(fm, slots, pmeta, chosen, rejected)


def place_kernel(where_ref, packed_ref, out_ref, src, onehot, outbuf, in_sems, out_sems):
    total, width = packed_ref.shape
    shard_rows = out_ref.shape[0]
    block_rows = shard_rows // BLOCKS
    padded = -(-block_rows // 16) * 16
    chunks = width // CHUNK
    slots = outbuf.shape[0]

    def fetch(c):
        return pltpu.make_async_copy(
            packed_ref.at[:, pl.ds(c * CHUNK, CHUNK)], src.at[c], in_sems.at[c]
        )

    def put(b, c, slot):
        return pltpu.make_async_copy(
            outbuf.at[slot, pl.ds(0, block_rows)],
            out_ref.at[pl.ds(b * block_rows, block_rows), pl.ds(c * CHUNK, CHUNK)],
            out_sems.at[slot],
        )

    for c in range(chunks):
        fetch(c).start()
    for b in range(BLOCKS):
        row_id = lax.broadcasted_iota(jnp.int32, (padded, WINDOW), 0) + b * block_rows
        target = where_ref[0:1, pl.ds(b * WINDOW, WINDOW)].astype(jnp.int32)
        onehot[...] = jnp.where(row_id == target, 1.0, 0.0).astype(jnp.bfloat16)
        for c in range(chunks):
            step = b * chunks + c
            if b == 0:
                fetch(c).wait()
            if step >= slots:
                put((step - slots) // chunks, (step - slots) % chunks, step % slots).wait()
            outbuf[step % slots] = jnp.dot(
                onehot[...], src[c, pl.ds(b * WINDOW, WINDOW), :],
                preferred_element_type=jnp.float32,
            ).astype(jnp.bfloat16)
            put(b, c, step % slots).start()
    steps = BLOCKS * chunks
    for step in range(steps - slots, steps):
        put(step // chunks, step % chunks, step % slots).wait()


def place_packed(shard_rows, where, packed):
    total, width = packed.shape
    chunks = width // CHUNK
    padded = -(-(shard_rows // BLOCKS) // 16) * 16
    vmem = pl.BlockSpec(memory_space=pltpu.VMEM)
    anyspec = pl.BlockSpec(memory_space=pl.ANY)
    return pl.pallas_call(
        place_kernel,
        out_shape=jax.ShapeDtypeStruct((shard_rows, width), packed.dtype),
        in_specs=[vmem, anyspec],
        out_specs=anyspec,
        scratch_shapes=[
            pltpu.VMEM((chunks, total, CHUNK), jnp.bfloat16),
            pltpu.VMEM((padded, WINDOW), jnp.bfloat16),
            pltpu.VMEM((4, padded, CHUNK), jnp.bfloat16),
            pltpu.SemaphoreType.DMA((chunks,)),
            pltpu.SemaphoreType.DMA((4,)),
        ],
        compiler_params=pltpu.CompilerParams(vmem_limit_bytes=48 * 1024 * 1024),
    )(where, packed)


def local(token_ids, sensitivity, last_hidden, lengths, norm_gain, reward_head,
          chosen_index, rejected_index, shard_owner):
    args = (token_ids, sensitivity, last_hidden, lengths, norm_gain, reward_head,
            chosen_index, rejected_index, shard_owner)
    resp_local, block_len = token_ids.shape
    devices = shard_owner.shape[0]
    n_grp, n_dev = lax.axis_size("grp"), lax.axis_size("dev")
    capacity = max(2, (2 * resp_local * block_len + devices - 1) // devices)
    shard_rows, width = VOCAB // devices, sensitivity.shape[2]
    if (capacity == NEAR and devices == 32 and n_grp in (1, 2, 4, 8) and n_dev % 4 == 0
            and resp_local == 4 and shard_rows % (8 * BLOCKS) == 0 and shard_rows < 64 * 250
            and width % CHUNK == 0 and width // devices <= 128):
        return relay_local(*args)
    prep = prepare(*args)
    return plain_finish(prep, n_dev)


def prepare(token_ids, sensitivity, last_hidden, lengths, norm_gain, reward_head,
            chosen_index, rejected_index, shard_owner):
    resp_local, block_len = token_ids.shape
    width = sensitivity.shape[2]
    tok_local = resp_local * block_len
    devices = shard_owner.shape[0]
    shard_rows = VOCAB // devices
    capacity = max(2, (2 * tok_local + devices - 1) // devices)
    hidden = last_hidden.astype(jnp.float32)
    normed = (
        hidden / jnp.sqrt(jnp.mean(hidden * hidden, axis=-1, keepdims=True) + 1e-05) * norm_gain
    )
    own_reward = jnp.sum(normed * reward_head, axis=-1)

    positions = jnp.arange(block_len, dtype=jnp.int32)
    live = (positions[None, :] < lengths[:, None]).reshape(tok_local)
    ids = token_ids.reshape(tok_local)
    shard_of = ids // shard_rows
    offset = ids - shard_of * shard_rows
    shard_hot = shard_of[:, None] == jnp.arange(devices, dtype=jnp.int32)[None, :]
    owner = jnp.sum(jnp.where(shard_hot, shard_owner[None, :], 0), axis=1)
    owner_hot = (owner[:, None] == jnp.arange(devices, dtype=jnp.int32)[None, :]) & live[:, None]
    live_hot = owner_hot.astype(jnp.bfloat16)
    token_pos = jnp.arange(tok_local, dtype=jnp.int32)
    earlier = (token_pos[:, None] > token_pos[None, :]).astype(jnp.bfloat16)
    before = jnp.dot(earlier, live_hot, preferred_element_type=jnp.float32)
    rank = jnp.sum(before * live_hot.astype(jnp.float32), axis=1).astype(jnp.int32)
    counts = jnp.sum(owner_hot.astype(jnp.int32), axis=0)
    return dict(
        sens=sensitivity.reshape(tok_local, width), normed=normed, own_reward=own_reward,
        live=live, offset=offset, owner=owner, rank=rank, counts=counts,
        owner_hot=owner_hot, resp=token_pos // block_len, capacity=capacity,
        chosen_index=chosen_index, rejected_index=rejected_index, devices=devices,
        shard_rows=shard_rows, resp_local=resp_local, width=width, tok_local=tok_local,
    )


def lane_pad(a, lanes):
    return jnp.pad(a, ((0, 0), (0, lanes - a.shape[1])))[:, None, :]


def reward_grads(p, reward):
    responses = p["devices"] * p["resp_local"]
    all_resp = jnp.arange(responses, dtype=jnp.int32)
    sign_table = (p["chosen_index"][:, None] == all_resp[None, :]).astype(jnp.float32) - (
        p["rejected_index"][:, None] == all_resp[None, :]
    ).astype(jnp.float32)
    margin = jnp.sum(sign_table * reward[None, :], axis=1)
    push = -jax.nn.sigmoid(-margin)
    return jnp.sum(sign_table * push[:, None], axis=0)


def place_all(shard_rows, rows, targets, scale):
    scaled = (scale[:, None] * rows).astype(jnp.bfloat16)
    placing = (targets[None, :] == jnp.arange(shard_rows, dtype=jnp.int32)[:, None]).astype(
        jnp.bfloat16
    )
    return jnp.dot(placing, scaled, preferred_element_type=jnp.float32).astype(jnp.bfloat16)


def plain_finish(p, n_dev):
    devices, capacity, resp_local = p["devices"], p["capacity"], p["resp_local"]
    width = p["width"]
    cols = width // devices
    responses = devices * resp_local
    lanes = -(-max(cols, capacity, resp_local) // 128) * 128
    slot = jnp.where(p["live"], p["owner"] * capacity + p["rank"], -1)
    slot_match = slot[None, :] == jnp.arange(devices * capacity, dtype=jnp.int32)[:, None]
    outgoing = jnp.dot(
        slot_match.astype(jnp.bfloat16), p["sens"], preferred_element_type=jnp.float32
    ).astype(jnp.bfloat16)
    code = (p["offset"] + 1) * resp_local + p["resp"]
    codes = jnp.sum(jnp.where(slot_match, code[None, :], 0), axis=1)
    codes = codes.reshape(devices, capacity)
    target_out = codes // resp_local - 1
    resp_out = codes - codes // resp_local * resp_local
    normed_blocks = p["normed"].reshape(resp_local, devices, cols).transpose(1, 0, 2)
    meta = jnp.concatenate(
        [
            lane_pad(target_out.astype(jnp.float32), lanes),
            lane_pad(resp_out.astype(jnp.float32), lanes),
            lane_pad(jnp.broadcast_to(p["own_reward"][None, :], (devices, resp_local)), lanes),
            jnp.zeros((devices, 1, lanes), jnp.float32),
            jnp.pad(normed_blocks, ((0, 0), (0, 0), (0, lanes - cols))),
        ],
        axis=1,
    )
    extra = -meta.shape[1] % 8
    meta = jnp.pad(meta, ((0, 0), (0, extra), (0, 0)))
    meta_in, arrived = exchange(
        meta, outgoing.reshape(devices, capacity, width), devices, n_dev
    )
    targets = meta_in[:, 0, :capacity].astype(jnp.int32).reshape(devices * capacity)
    resp_in = meta_in[:, 1, :capacity].astype(jnp.int32)
    reward = meta_in[:, 2, :resp_local].reshape(responses)
    normed_in = meta_in[:, 4 : 4 + resp_local, :cols]
    reward_grad = reward_grads(p, reward).reshape(devices, resp_local)
    head_grad = jnp.sum(reward_grad[:, :, None] * normed_in, axis=(0, 1))
    resp_hot = resp_in[:, :, None] == jnp.arange(resp_local, dtype=jnp.int32)[None, None, :]
    scale = jnp.sum(jnp.where(resp_hot, reward_grad[:, None, :], 0.0), axis=2)
    total = devices * capacity
    owned = place_all(
        p["shard_rows"], arrived.reshape(total, width), targets, scale.reshape(total)
    )
    return owned, head_grad


def relay_local(*args):
    n_grp, n_dev = lax.axis_size("grp"), lax.axis_size("dev")
    p = prepare(*args)
    devices, resp_local, width = p["devices"], p["resp_local"], p["width"]
    hd = n_dev // 2
    local_n = devices // 2
    pieces = n_grp + 1
    cols = width // devices
    g, v = lax.axis_index("grp"), lax.axis_index("dev")
    half = v // hd
    u = v % hd
    me = g * n_dev + v
    owner, rank, live = p["owner"], p["rank"], p["live"]
    owner_g, owner_v = owner // n_dev, owner % n_dev
    owner_u = owner_v % hd
    away = (owner_g - g) % n_grp * hd + (owner_u - u) % hd
    near = owner_v // hd == half
    dev_ids = jnp.arange(devices, dtype=jnp.int32)
    dev_far = dev_ids % n_dev // hd != half
    over = jnp.where(dev_far, jnp.maximum(p["counts"] - FAR, 0), 0)
    over_base = jnp.sum(jnp.where(dev_ids[None, :] < dev_ids[:, None], over[None, :], 0), axis=1)
    j = jnp.sum(jnp.where(p["owner_hot"], over_base[None, :], 0), axis=1) + rank - FAR
    far_start = local_n * NEAR
    piece_start = far_start + local_n * FAR
    slots = piece_start + pieces * GROUP
    piece_slot = jnp.where(
        j < pieces * GROUP, piece_start + j % pieces * GROUP + j // pieces, -1
    )
    slot = jnp.where(
        near,
        away * NEAR + rank,
        jnp.where(rank < FAR, far_start + away * FAR + rank, piece_slot),
    )
    slot = jnp.where(live, slot, -1)
    slot_match = slot[None, :] == jnp.arange(slots, dtype=jnp.int32)[:, None]
    outgoing = jnp.dot(
        slot_match.astype(jnp.bfloat16), p["sens"], preferred_element_type=jnp.float32
    ).astype(jnp.bfloat16)
    code = (p["offset"] + 1) * 128 + me * resp_local + p["resp"]
    lane_at = jnp.where(near, away % 4 * NEAR, away % 8 * FAR) + rank
    shown = live & (near | (rank < FAR))
    direct = jnp.where(shown, owner * 128 + lane_at, -1)
    direct_match = direct[None, :] == jnp.arange(devices * 128, dtype=jnp.int32)[:, None]
    codes = jnp.sum(jnp.where(direct_match, code[None, :], 0), axis=1).reshape(devices, 1, 128)
    piece_match = slot_match[piece_start:]
    piece_code = jnp.sum(jnp.where(piece_match, code[None, :], 0), axis=1)
    piece_owner = jnp.sum(
        jnp.where(piece_match, (owner_g * hd + owner_u)[None, :], 0), axis=1
    )
    piece_target = piece_code // 128
    lane = jnp.arange(128, dtype=jnp.int32)[None, :]
    pmeta = jnp.zeros((pieces * GROUP, 128), jnp.int32)
    for i, col in enumerate(
        (
            (piece_code > 0).astype(jnp.int32),
            piece_owner // hd,
            piece_owner % hd,
            piece_code % 128,
            piece_target // 64,
            piece_target % 64,
        )
    ):
        pmeta = jnp.where(lane == i, col[:, None], pmeta)
    pmeta = pmeta.astype(jnp.float32).reshape(pieces, GROUP, 128)
    normed_blocks = p["normed"].reshape(resp_local, devices, cols).transpose(1, 0, 2)
    reward_lane = jnp.arange(128, dtype=jnp.int32)[None, :] - me * resp_local
    reward_row = jnp.sum(
        jnp.where(
            reward_lane == jnp.arange(resp_local, dtype=jnp.int32)[:, None],
            p["own_reward"][:, None], 0.0,
        ),
        axis=0,
    )
    fm = jnp.concatenate(
        [
            jnp.broadcast_to(reward_row[None, None, :], (devices, 1, 128)),
            codes.astype(jnp.float32),
            lane_pad(jnp.broadcast_to(over.astype(jnp.float32)[None, :], (devices, devices)), 128),
            jnp.zeros((devices, 1, 128), jnp.float32),
            jnp.pad(normed_blocks, ((0, 0), (0, 4 - resp_local), (0, 128 - cols))),
        ],
        axis=1,
    )
    rows_in, packed, where, slot_info, head, flag = relay_exchange(
        fm, outgoing, pmeta, p["chosen_index"][:, None], p["rejected_index"][:, None],
        n_grp, n_dev, p["shard_rows"] // BLOCKS,
    )

    def relayed(operands):
        rows, packed, where, slot_info, flag = operands

        def spread(o):
            return place_all(
                p["shard_rows"], o[0], o[3][:, 0].reshape(-1).astype(jnp.int32),
                o[3][:, 1].reshape(-1),
            )

        return lax.cond(
            flag[1, 0] <= 0.0,
            lambda o: place_packed(p["shard_rows"], o[2], o[1]),
            spread,
            (rows, packed, where, slot_info),
        )

    owned = lax.cond(
        flag[0, 0] <= 0.0,
        relayed,
        lambda operands: plain_finish(p, n_dev)[0],
        (rows_in, packed, where, slot_info, flag),
    )
    return owned, head[0, :cols]


def solution(mesh):
    placed = (
        P(("grp", "dev"), None),
        P(("grp", "dev"), None, None),
        P(("grp", "dev"), None),
        P(("grp", "dev")),
        P(),
        P(),
        P(),
        P(),
        P(),
    )
    return jax.shard_map(
        local,
        mesh=mesh,
        in_specs=placed,
        out_specs=(P(("grp", "dev"), None), P(("grp", "dev"))),
        check_vma=False,
    )
```

time: 215 us -> 170 us (0.79)
  matrix products: 37.5 us -> 8.02 us
  other arithmetic: 16.9 us -> 8.1 us
  Pallas kernels: 152 us -> 145 us
  local copies, waits for them, and re-layouts: 3.49 us -> 6.6 us
    dot_general x3 -> x0, matrix products: 29.5 us -> none  [the longest x1 17.4 us: packed_place(): lax.dot_general(placing.astype(jnp.bfloat16), packed.reshape(blocks, wind...]
    pallas_call x1 -> x2, Pallas kernels: 152 us -> 145 us  [the longest x1 130 us: relay_exchange(): pl.pallas_call(functools.partial(relay_kernel, n_grp, n_dev, block_rows),...]
    reduce_sum x16 -> x2, other arithmetic: 5.81 us -> 0.21 us  [the longest x1 0.12 us: relay_local(): jnp.sum(jnp.where(piece_match, (owner_g * hd + owner_u)[None, :], 0), axi...]
    broadcast_in_dim x0 -> x3, local copies, waits for them, and re-layouts: none -> 2.71 us  [the longest x1 1.35 us: relay_local(): p['rejected_index'][:, None]]
where the time goes in v3:
time: 170 us
  Pallas kernels  145 us (85%)
  other arithmetic  8.1 us (5%)
  matrix products  8.02 us (5%)
  local copies, waits for them, and re-layouts  6.6 us (4%)
    pallas_call x1, Pallas kernels, relay_exchange(): pl.pallas_call(functools.partial(relay_kernel, n_grp, n_dev, block_rows),...  130 us
    pallas_call x1, Pallas kernels, place_packed(): pl.pallas_call(place_kernel, out_shape=jax.ShapeDtypeStruct((shard_rows,...  14.9 us
    dot_general x1, matrix products, relay_local(): jnp.dot(slot_match.astype(jnp.bfloat16), p['sens'], preferred_element_typ...  7.74 us

profile of v3, /device:TPU:11, one launch (start us, length us, event | category | flops | bytes accessed | tf_op | source)
XLA Modules:
  0.0 169.5 jit_solution(7481466346371165403)
XLA Ops:
  0.7 0.7 fusion.48
  1.4 0.9 fusion.18
  2.3 0.7 lt.128
  3.1 0.7 broadcast_divide_fusion
  3.8 0.7 select_reduce_fusion.6
  4.5 0.1 convert_reduce_fusion.2
  4.9 0.3 fusion.16
  5.2 0.7 select_select_fusion
  5.9 0.7 multiply_add_fusion
  6.6 1.0 select_reduce_fusion.2
  7.6 1.4 copy.20.rejected_ref
  9.0 1.3 copy.19.chosen_ref
  10.3 1.0 multiply_reduce_fusion.2
  11.5 0.8 concatenate.6.fm_ref
  12.2 0.3 iota_compare_fusion.10
  12.8 0.7 select_convert_fusion.pmeta_ref
  13.5 7.7 %convolution_convert_fusion.3.slots_ref = bf16[808,4096]{1,0:T(8,128)(2,1)} fusion(bf16[512,4096]{1,0:T(8,128)(2,1)} %bitcast.55, s32[512]{0:T(512)S(1)} %get-tuple-element.182), kind=kOutput, calls=%fused_computation.53 | convolution fusion | flops 3392720896 | bytes 10815488 | tf_op jit(solution)/shard_map/dot_general | solution.py:730
  21.3 129.7 %shard_map.104 = (bf16[896,4096]{1,0:T(8,128)(2,1)}, bf16[768,4096]{1,0:T(8,128)(2,1)}, f32[8,768]{1,0:T(8,128)S(1)}, f32[7,8,128]{2,1,0:T(8,128)S(1)}, f32[8,128]{1,0:T(8,128)}, /*index=5*/f32[8,128]{1,0:T(8,128)S(1)}) custom-call(f32[32,8,128]{2,1,0:T(8,128)} %concatenate.6.fm_ref, bf16[808,4096]{1,0:T(8,128)(2,1)} %convolution_convert_fusion.3.slots_ref, ...), custom_call_target="tpu_custom_call" | custom-call | tf_op jit(solution)/shard_map/pallas_call | solution.py:466
  150.9 0.5 slice.31
  152.1 1.2 slice_bitcast_fusion
  153.3 16.0 %conditional.2 = (bf16[4008,4096]{1,0:T(8,128)(2,1)}) conditional(s32[]{:T(128)} %bitcast.18, (s32[4,128]{1,0:T(4,128)S(1)}, s32[4,128]{1,0:T(4,128)S(1)}, s32[512]{0:T(512)S(1)}, s32[512]{0:T(512)S(1)}, s32[512]{0:T(512)S(1)}, /*index=5*/s32[512]{0:T(512)S(1)}, s32[512]{0:T(512)S(1)}, s32[512]{0:T(512)S(1)}, s32[512]{0:T(512)S(1)}, ...), branch_computations={%region_11.16_spmd, %region_16.19_spmd} | conditional | flops 37956063232 | bytes 54258216 | solution.py:799
  153.3 0.5 slice.26
  154.5 14.9 %conditional = (bf16[4008,4096]{1,0:T(8,128)(2,1)}) conditional(s32[]{:T(128)} %bitcast.9, (f32[7,8,128]{2,1,0:T(8,128)S(1)}, bf16[896,4096]{1,0:T(8,128)(2,1)}) %tuple.16, (f32[8,768]{1,0:T(8,128)S(1)}, bf16[768,4096]{1,0:T(8,128)(2,1)}) %tuple.17), branch_computations={%region_17.17_spmd, %region_18.18_spmd} | conditional | flops 29449867264 | bytes 40195080 | solution.py:792
  154.5 14.9 %branch_1_fun.1 = bf16[4008,4096]{1,0:T(8,128)(2,1)} custom-call(f32[8,768]{1,0:T(8,128)S(1)} %get-tuple-element.159.where_ref, bf16[768,4096]{1,0:T(8,128)(2,1)} %get-tuple-element.160.packed_ref), custom_call_target="tpu_custom_call" | custom-call | tf_op jit(solution)/shard_map/cond/branch_1_fun/cond/branch_1_fun/pallas_call | solution.py:555
  (33 shorter events, 0.7 us)
Async XLA Ops:
  13.5 138.6 %copy-start = (s32[4,128]{1,0:T(4,128)S(1)}, s32[4,128]{1,0:T(4,128)}, u32[]{:S(2)}) copy-start(s32[4,128]{1,0:T(4,128)} %param.13) | copy-start | bytes 6148
  13.5 138.6 %copy-start.1 = (s32[64]{0:T(128)S(1)}, s32[64]{0:T(128)}, u32[]{:S(2)}) copy-start(s32[64]{0:T(128)} %param.19) | copy-start | bytes 772
  13.5 138.6 %copy-start.2 = (s32[64]{0:T(128)S(1)}, s32[64]{0:T(128)}, u32[]{:S(2)}) copy-start(s32[64]{0:T(128)} %param.20) | copy-start | bytes 772

commit v4 on v3

--- a/solution.py
+++ b/solution.py
@@ -91,6 +91,7 @@
 NEAR = 32
 FAR = 16
 FWD = 8
+AHEAD = 4
 WINDOW = 256
 BLOCKS = 3
 CHUNK = 512
@@ -106,11 +107,17 @@
     return 256 + k * FAR + (k // EARLY) * 128
 
 
-def relay_kernel(n_grp, n_dev, block_rows, fm_ref, slots_ref, pmeta_ref, chosen_ref,
-                 rejected_ref, rows_out, packed_out, where_out, slot_out, head_out, flag_out,
+def log2(x):
+    return x.bit_length() - 1
+
+
+def relay_kernel(n_grp, n_dev, block_rows, ids_ref, sens_ref, hidden_ref, length_ref, gain_ref,
+                 weight_ref, chosen_ref, rejected_ref, owner_ref,
+                 rows_out, packed_out, where_out, slot_out, head_out, flag_out,
+                 sens_v, select, slots_v, pout, fm_out, pmeta_out,
                  rin, fin, fm_in, pin, pmeta_in, fwd, fwd_meta, fmeta_in, picks, scales, packed,
-                 fm_sems, near_sems, far_sems, piece_sems, pm_sems, fwd_sems, fwdm_sems,
-                 own_sems, save_sems, pack_sems):
+                 sens_sems, fm_sems, near_sems, far_sems, piece_sems, pm_sems, fwd_sems,
+                 fwdm_sems, save_sems, pack_sems):
     g = lax.axis_index("grp")
     v = lax.axis_index("dev")
     hd = n_dev // 2
@@ -123,8 +130,16 @@
     direct = local_n * (NEAR + FAR)
     far_base = local_n * NEAR
     other = 1 - half
-    width = slots_ref.shape[1]
+    width = sens_ref.shape[1]
     f32 = jnp.float32
+    chunks = width // CHUNK
+    count = pieces * GROUP
+    shard_rows = block_rows * BLOCKS
+    i32 = jnp.int32
+    rows_rows = (((1,), (1,)), ((), ()))
+
+    def iota(rows, cols, axis):
+        return lax.broadcasted_iota(i32, (rows, cols), axis)
 
     def coord(t):
         return (t // n_dev, lax.rem(t, n_dev))
@@ -138,14 +153,124 @@
         return c
 
     lax.fori_loop(1, n, greet, 0)
-    own = [
-        pltpu.make_async_copy(fm_ref.at[me], fm_in.at[0], own_sems.at[0]),
-        pltpu.make_async_copy(
-            slots_ref.at[pl.ds(0, NEAR)], rin.at[pl.ds(0, NEAR)], own_sems.at[1]
-        ),
-    ]
-    for cp in own:
-        cp.start()
+    def fetch(c):
+        return pltpu.make_async_copy(
+            sens_ref.at[:, pl.ds(c * CHUNK, CHUNK)], sens_v.at[c], sens_sems.at[c]
+        )
+
+    for c in range(chunks):
+        fetch(c).start()
+
+    eye0, eye1 = iota(128, 128, 0), iota(128, 128, 1)
+    tri = jnp.where(eye0 < eye1, 1.0, 0.0)
+    resp_local, block_len = ids_ref.shape
+    resp_row, resp_pos = iota(resp_local, block_len, 0), iota(resp_local, block_len, 1)
+    ids = ids_ref[...]
+    length = jnp.zeros((resp_local, block_len), i32)
+    for r in range(resp_local):
+        length = jnp.where(resp_row == r, length_ref[r], length)
+    live_all = resp_pos < length
+    shard = jnp.floor((ids.astype(f32) + 0.5) * (1.0 / shard_rows)).astype(i32)
+    above = ids - shard * shard_rows + 1
+    owner_all = jnp.zeros((resp_local, block_len), i32)
+    for k in range(n):
+        owner_all = jnp.where(shard == k, owner_ref[k], owner_all)
+    owner_g = owner_all >> log2(n_dev)
+    owner_v = owner_all & (n_dev - 1)
+    owner_u = owner_v & (hd - 1)
+    near_all = (owner_v >> log2(hd)) == half
+    away_all = (((owner_g - g) & (n_grp - 1)) << log2(hd)) + ((owner_u - u) & (hd - 1))
+    dev_row = iota(n, 128, 0)
+    filled_to = jnp.zeros((n, 1), f32)
+    hots, ranks = [], []
+    for r in range(resp_local):
+        live = live_all[r : r + 1]
+        hot = jnp.where((dev_row == owner_all[r : r + 1]) & live, 1.0, 0.0)
+        ahead = jnp.dot(hot, tri, preferred_element_type=f32) + filled_to
+        ranks.append(jnp.sum(hot * ahead, axis=0, keepdims=True))
+        filled_to = filled_to + jnp.sum(hot, axis=1, keepdims=True)
+        hots.append(hot)
+    dev_far = ((dev_row & (n_dev - 1)) >> log2(hd)) != half
+    over_out = jnp.where(dev_far, jnp.maximum(filled_to - FAR, 0.0), 0.0)
+    lower = jnp.where(iota(n, n, 0) > iota(n, n, 1), 1.0, 0.0)
+    base_out = jnp.dot(lower, over_out, preferred_element_type=f32)
+    over_row = jnp.sum(
+        jnp.where(dev_row == iota(n, 128, 1), over_out, 0.0), axis=0, keepdims=True
+    )
+    code_hi = jnp.zeros((n, 128), f32)
+    code_lo = jnp.zeros((n, 128), f32)
+    code_resp = jnp.zeros((n, 128), f32)
+    piece_meta = jnp.zeros((count, 128), f32)
+    for r in range(resp_local):
+        live, near = live_all[r : r + 1], near_all[r : r + 1]
+        away, rank = away_all[r : r + 1], ranks[r]
+        place_j = jnp.sum(hots[r] * base_out, axis=0, keepdims=True) + rank - FAR
+        level = jnp.floor((place_j + 0.5) * (1.0 / pieces))
+        piece = direct + (place_j - pieces * level) * GROUP + level
+        piece = jnp.where(place_j < count, piece, -1.0).astype(i32)
+        rank = rank.astype(i32)
+        slot = jnp.where(
+            near,
+            away * NEAR + rank,
+            jnp.where(rank < FAR, far_base + away * FAR + rank, piece),
+        )
+        slot = jnp.where(live, slot, -1)
+        select[:, pl.ds(r * 128, 128)] = jnp.where(
+            iota(direct + 48, 128, 0) == slot, 1.0, 0.0
+        ).astype(jnp.bfloat16)
+        lane_at = jnp.where(near, (away & 3) * NEAR, (away & 7) * FAR) + rank
+        shown = live & (near | (rank < FAR))
+        at_hot = jnp.where(eye0 == jnp.where(shown, lane_at, -1), 1.0, 0.0)
+        hi = (above[r : r + 1] >> 6).astype(f32)
+        lo = (above[r : r + 1] & 63).astype(f32)
+        resp = (iota(1, 128, 1) * 0 + (me * resp_local + r)).astype(f32)
+        code_hi += lax.dot_general(hots[r] * hi, at_hot, rows_rows, preferred_element_type=f32)
+        code_lo += lax.dot_general(hots[r] * lo, at_hot, rows_rows, preferred_element_type=f32)
+        code_resp += lax.dot_general(
+            hots[r] * resp, at_hot, rows_rows, preferred_element_type=f32
+        )
+        feature = jnp.where(eye0 == 0, 1.0, 0.0)
+        for i, row in (
+            (1, owner_g[r : r + 1].astype(f32)), (2, owner_u[r : r + 1].astype(f32)),
+            (3, resp), (4, hi), (5, lo),
+        ):
+            feature = jnp.where(eye0 == i, row, feature)
+        in_piece = jnp.where(iota(count, 128, 0) + direct == slot, 1.0, 0.0)
+        piece_meta += lax.dot_general(
+            in_piece, feature, rows_rows, preferred_element_type=f32
+        )
+    pmeta_out[...] = piece_meta.reshape(pieces, GROUP, 128)
+
+    hidden = hidden_ref[...].astype(f32)
+    square = jnp.sum(hidden * hidden, axis=1, keepdims=True) * (1.0 / width)
+    normed = hidden / jnp.sqrt(square + 1e-05) * gain_ref[...]
+    own_reward = jnp.sum(normed * weight_ref[...], axis=1, keepdims=True)
+    reward_row = jnp.sum(
+        jnp.where(resp_pos == me * resp_local + resp_row, own_reward, 0.0),
+        axis=0, keepdims=True,
+    )
+    fm_out[:, 0, :] = jnp.broadcast_to(reward_row, (n, 128))
+    fm_out[:, 1, :] = (code_hi * 64.0 + code_lo) * 128.0 + code_resp
+    fm_out[:, 2, :] = jnp.broadcast_to(over_row, (n, 128))
+    fm_out[:, 3, :] = jnp.zeros((n, 128), f32)
+    for d in range(n):
+        fm_out[d, 4:8, :] = normed[:, d * 128 : (d + 1) * 128]
+    fm_in[0] = fm_out[me]
+
+    def build_far(c, carry):
+        cols = pl.ds(pl.multiple_of(c * CHUNK, CHUNK), CHUNK)
+        fetch(c).wait()
+        got = jnp.dot(select[pl.ds(far_base, direct + 48 - far_base), :], sens_v[c],
+                      preferred_element_type=f32)
+        slots_v[pl.ds(far_base, direct - far_base), cols] = got[
+            : direct - far_base
+        ].astype(jnp.bfloat16)
+        pout[:, :, cols] = got[direct - far_base : direct - far_base + count].reshape(
+            pieces, GROUP, CHUNK
+        ).astype(jnp.bfloat16)
+        return carry
+
+    lax.fori_loop(0, chunks, build_far, 0)
     pl.semaphore_wait(barrier, n - 1)
 
     def remote(src, dst, send_sem, recv_sem, to):
@@ -166,11 +291,11 @@
     for q in range(pieces):
         to = piece_target(q)
         piece_copies.append(
-            remote(slots_ref.at[pl.ds(direct + q * GROUP, GROUP)], pin.at[q],
+            remote(pout.at[q], pin.at[q],
                    piece_sems.at[0, q], piece_sems.at[1, q], to)
         )
         piece_copies.append(
-            remote(pmeta_ref.at[q], pmeta_in.at[q], pm_sems.at[0, q], pm_sems.at[1, q], to)
+            remote(pmeta_out.at[q], pmeta_in.at[q], pm_sems.at[0, q], pm_sems.at[1, q], to)
         )
     for cp in piece_copies:
         cp.start()
@@ -178,18 +303,18 @@
     def fm_copy(r):
         side = lax.rem(half + r // local_n, 2)
         tg, tv = partner(lax.rem(r, local_n), side)
-        return remote(fm_ref.at[tg * n_dev + tv], fm_in.at[r], fm_sems.at[0, r],
+        return remote(fm_out.at[tg * n_dev + tv], fm_in.at[r], fm_sems.at[0, r],
                       fm_sems.at[1, r], (tg, tv))
 
     def near_copy(k):
         return remote(
-            slots_ref.at[pl.ds(k * NEAR, NEAR)], rin.at[pl.ds(near_row(k), NEAR)],
+            slots_v.at[pl.ds(k * NEAR, NEAR)], rin.at[pl.ds(near_row(k), NEAR)],
             near_sems.at[0, k], near_sems.at[1, k], partner(k, half),
         )
 
     def far_copy(k):
         return remote(
-            slots_ref.at[pl.ds(far_base + k * FAR, FAR)], rin.at[pl.ds(far_row(k), FAR)],
+            slots_v.at[pl.ds(far_base + k * FAR, FAR)], rin.at[pl.ds(far_row(k), FAR)],
             far_sems.at[0, k], far_sems.at[1, k], partner(k, other),
         )
 
@@ -205,18 +330,36 @@
         return c
 
     lax.fori_loop(1, n, send_fm, 0)
-    far_copy(0).start()
+
+    def send_far(k, c):
+        far_copy(k).start()
+        return c
 
     def send_both(k, c):
         far_copy(k).start()
         near_copy(k).start()
         return c
 
-    lax.fori_loop(1, local_n, send_both, 0)
+    def send_near(k, c):
+        near_copy(k).start()
+        return c
+
+    lax.fori_loop(0, AHEAD, send_far, 0)
+
+    def build_near(c, carry):
+        cols = pl.ds(pl.multiple_of(c * CHUNK, CHUNK), CHUNK)
+        got = jnp.dot(select[pl.ds(0, far_base), :], sens_v[c],
+                      preferred_element_type=f32).astype(jnp.bfloat16)
+        slots_v[pl.ds(0, far_base), cols] = got
+        rin[pl.ds(0, NEAR), cols] = got[:NEAR]
+        return carry
+
+    lax.fori_loop(0, chunks, build_near, 0)
+    lax.fori_loop(1, AHEAD, send_near, 0)
+    lax.fori_loop(AHEAD, local_n, send_both, 0)
 
     for cp in piece_copies:
         cp.wait_recv()
-    count = pieces * GROUP
     marks = pmeta_in[...].reshape(count, 128)
     used = marks[:, 0:1] > 0.0
     dst_g = marks[:, 1:2].astype(jnp.int32)
@@ -232,7 +375,6 @@
     slot = jnp.where(used & (rank < FWD), dst * FWD + rank, -1)
     place = jnp.where(lane == slot, 1.0, 0.0)
     contract = (((0,), (0,)), ((), ()))
-    rows_rows = (((1,), (1,)), ((), ()))
 
     def gather(c, carry):
         cols = pl.ds(pl.multiple_of(c * CHUNK, CHUNK), CHUNK)
@@ -262,7 +404,6 @@
         cp.wait_recv()
         return c
 
-    own[0].wait()
     lax.fori_loop(1, n, wait_fm, 0)
 
     def source(r):
@@ -273,15 +414,19 @@
 
     reward = jnp.sum(fm_in[:, 0, :], axis=0, keepdims=True)
     pairs = chosen_ref.shape[0]
-    pair_lane = lax.broadcasted_iota(jnp.int32, (pairs, 128), 1)
-    sign = jnp.where(chosen_ref[...] == pair_lane, 1.0, 0.0) - jnp.where(
-        rejected_ref[...] == pair_lane, 1.0, 0.0
+    pair_row = iota(pairs, 1, 0)
+    chosen = jnp.zeros((pairs, 1), i32)
+    rejected = jnp.zeros((pairs, 1), i32)
+    for k in range(pairs):
+        chosen = jnp.where(pair_row == k, chosen_ref[k], chosen)
+        rejected = jnp.where(pair_row == k, rejected_ref[k], rejected)
+    pair_lane = iota(pairs, 128, 1)
+    sign = jnp.where(chosen == pair_lane, 1.0, 0.0) - jnp.where(
+        rejected == pair_lane, 1.0, 0.0
     )
     margin = jnp.sum(sign * reward, axis=1, keepdims=True)
     push = -1.0 / (1.0 + jnp.exp(margin))
     reward_grad = jnp.sum(sign * push, axis=0, keepdims=True)
-    eye0 = lax.broadcasted_iota(jnp.int32, (128, 128), 0)
-    eye1 = lax.broadcasted_iota(jnp.int32, (128, 128), 1)
     grad_col = jnp.sum(jnp.where(eye0 == eye1, reward_grad, 0.0), axis=1, keepdims=True)
     src_lane = lax.broadcasted_iota(jnp.int32, (n, 128), 1)
     _, _, src = source(lax.broadcasted_iota(jnp.int32, (n, 128), 0))
@@ -290,11 +435,10 @@
         part = jnp.where(src_lane == src * 4 + j, reward_grad, 0.0)
         coef = jnp.sum(part, axis=1, keepdims=True)
         head = head + jnp.sum(coef * fm_in[:, 4 + j, :], axis=0, keepdims=True)
-    head_out[...] = jnp.broadcast_to(head, (8, 128))
+    head_out[...] = head
 
     over = fm_in[:, 2, :]
-    upper = jnp.where(eye0 < eye1, 1.0, 0.0)
-    over_base = jnp.dot(over, upper, preferred_element_type=f32)
+    over_base = jnp.dot(over, tri, preferred_element_type=f32)
     here = lax.broadcasted_iota(jnp.int32, (local_n, n), 0)
     from_g, from_u, _ = source(lax.broadcasted_iota(jnp.int32, (local_n, n), 1))
     load = jnp.zeros((local_n, 128), f32)
@@ -320,7 +464,6 @@
         code_row(0, 4), code_row(4, 4), code_row(local_n, 8),
         code_row(8, 4), code_row(local_n + 8, 8), code_row(12, 4),
     ]
-    tri = jnp.where(eye0 < eye1, 1.0, 0.0)
     sub = lax.broadcasted_iota(jnp.int32, (8, 128), 0)
     resp_id = eye0
     total = packed.shape[0]
@@ -394,7 +537,6 @@
         cp.wait_recv()
         return c
 
-    own[1].wait()
     saves = [save(i, rin.at[pl.ds(i * 256, 256)], i * 256, 256) for i in range(3)]
     lax.fori_loop(1, EARLY, wait_near, 0)
     saves[0].start()
@@ -451,16 +593,18 @@
         pack_out(c).wait()
 
 
-def relay_exchange(fm, slots, pmeta, chosen, rejected, n_grp, n_dev, block_rows):
+def relay_exchange(args, n_grp, n_dev, block_rows):
+    ids, sens, hidden, lengths, gain, weight, chosen, rejected, owner = args
+    resp_local, block_len, width = sens.shape
     n = n_grp * n_dev
     local_n = n // 2
-    width = slots.shape[1]
     pieces = n_grp + 1
     direct = local_n * (NEAR + FAR)
     rows = direct + local_n * FWD
     total = BLOCKS * WINDOW
     anyspec = pl.BlockSpec(memory_space=pl.ANY)
     vmem = pl.BlockSpec(memory_space=pltpu.VMEM)
+    smem = pl.BlockSpec(memory_space=pltpu.SMEM)
     sem = pltpu.SemaphoreType.DMA
     bf16, f32 = jnp.bfloat16, jnp.float32
     return pl.pallas_call(
@@ -470,12 +614,18 @@
             jax.ShapeDtypeStruct((total, width), bf16),
             jax.ShapeDtypeStruct((8, total), f32),
             jax.ShapeDtypeStruct((rows // 128, 8, 128), f32),
-            jax.ShapeDtypeStruct((8, 128), f32),
+            jax.ShapeDtypeStruct((1, 128), f32),
             jax.ShapeDtypeStruct((8, 128), f32),
         ),
-        in_specs=[anyspec, anyspec, anyspec, vmem, vmem],
+        in_specs=[vmem, anyspec, vmem, smem, vmem, vmem, smem, smem, smem],
         out_specs=(anyspec, anyspec, vmem, vmem, vmem, vmem),
         scratch_shapes=[
+            pltpu.VMEM((width // CHUNK, resp_local * block_len, CHUNK), bf16),
+            pltpu.VMEM((direct + 48, resp_local * block_len), bf16),
+            pltpu.VMEM((direct, width), bf16),
+            pltpu.VMEM((pieces, GROUP, width), bf16),
+            pltpu.VMEM((n, 8, 128), f32),
+            pltpu.VMEM((pieces, GROUP, 128), f32),
             pltpu.VMEM((direct, width), bf16),
             pltpu.VMEM((local_n, FWD, width), bf16),
             pltpu.VMEM((n, 8, 128), f32),
@@ -487,6 +637,7 @@
             pltpu.VMEM((rows // 128, total, 128), bf16),
             pltpu.VMEM((4, total, 1), f32),
             pltpu.VMEM((total, width), bf16),
+            sem((width // CHUNK,)),
             sem((2, n)),
             sem((2, local_n)),
             sem((2, local_n)),
@@ -494,14 +645,14 @@
             sem((2, pieces)),
             sem((2, local_n)),
             sem((2, local_n)),
-            sem((2,)),
             sem((3 + local_n,)),
             sem((width // CHUNK,)),
         ],
         compiler_params=pltpu.CompilerParams(
             collective_id=0, has_side_effects=True, vmem_limit_bytes=56 * 1024 * 1024
         ),
-    )(fm, slots, pmeta, chosen, rejected)
+    )(ids, sens.reshape(-1, width), hidden, lengths, gain[None, :], weight[None, :], chosen,
+      rejected, owner)
 
 
 def place_kernel(where_ref, packed_ref, out_ref, src, onehot, outbuf, in_sems, out_sems):
@@ -579,7 +730,7 @@
     shard_rows, width = VOCAB // devices, sensitivity.shape[2]
     if (capacity == NEAR and devices == 32 and n_grp in (1, 2, 4, 8) and n_dev % 4 == 0
             and resp_local == 4 and shard_rows % (8 * BLOCKS) == 0 and shard_rows < 64 * 250
-            and width % CHUNK == 0 and width // devices <= 128):
+            and width % CHUNK == 0 and width // devices == 128 and block_len == 128):
         return relay_local(*args)
     prep = prepare(*args)
     return plain_finish(prep, n_dev)
@@ -694,90 +845,9 @@
 
 def relay_local(*args):
     n_grp, n_dev = lax.axis_size("grp"), lax.axis_size("dev")
-    p = prepare(*args)
-    devices, resp_local, width = p["devices"], p["resp_local"], p["width"]
-    hd = n_dev // 2
-    local_n = devices // 2
-    pieces = n_grp + 1
-    cols = width // devices
-    g, v = lax.axis_index("grp"), lax.axis_index("dev")
-    half = v // hd
-    u = v % hd
-    me = g * n_dev + v
-    owner, rank, live = p["owner"], p["rank"], p["live"]
-    owner_g, owner_v = owner // n_dev, owner % n_dev
-    owner_u = owner_v % hd
-    away = (owner_g - g) % n_grp * hd + (owner_u - u) % hd
-    near = owner_v // hd == half
-    dev_ids = jnp.arange(devices, dtype=jnp.int32)
-    dev_far = dev_ids % n_dev // hd != half
-    over = jnp.where(dev_far, jnp.maximum(p["counts"] - FAR, 0), 0)
-    over_base = jnp.sum(jnp.where(dev_ids[None, :] < dev_ids[:, None], over[None, :], 0), axis=1)
-    j = jnp.sum(jnp.where(p["owner_hot"], over_base[None, :], 0), axis=1) + rank - FAR
-    far_start = local_n * NEAR
-    piece_start = far_start + local_n * FAR
-    slots = piece_start + pieces * GROUP
-    piece_slot = jnp.where(
-        j < pieces * GROUP, piece_start + j % pieces * GROUP + j // pieces, -1
-    )
-    slot = jnp.where(
-        near,
-        away * NEAR + rank,
-        jnp.where(rank < FAR, far_start + away * FAR + rank, piece_slot),
-    )
-    slot = jnp.where(live, slot, -1)
-    slot_match = slot[None, :] == jnp.arange(slots, dtype=jnp.int32)[:, None]
-    outgoing = jnp.dot(
-        slot_match.astype(jnp.bfloat16), p["sens"], preferred_element_type=jnp.float32
-    ).astype(jnp.bfloat16)
-    code = (p["offset"] + 1) * 128 + me * resp_local + p["resp"]
-    lane_at = jnp.where(near, away % 4 * NEAR, away % 8 * FAR) + rank
-    shown = live & (near | (rank < FAR))
-    direct = jnp.where(shown, owner * 128 + lane_at, -1)
-    direct_match = direct[None, :] == jnp.arange(devices * 128, dtype=jnp.int32)[:, None]
-    codes = jnp.sum(jnp.where(direct_match, code[None, :], 0), axis=1).reshape(devices, 1, 128)
-    piece_match = slot_match[piece_start:]
-    piece_code = jnp.sum(jnp.where(piece_match, code[None, :], 0), axis=1)
-    piece_owner = jnp.sum(
-        jnp.where(piece_match, (owner_g * hd + owner_u)[None, :], 0), axis=1
-    )
-    piece_target = piece_code // 128
-    lane = jnp.arange(128, dtype=jnp.int32)[None, :]
-    pmeta = jnp.zeros((pieces * GROUP, 128), jnp.int32)
-    for i, col in enumerate(
-        (
-            (piece_code > 0).astype(jnp.int32),
-            piece_owner // hd,
-            piece_owner % hd,
-            piece_code % 128,
-            piece_target // 64,
-            piece_target % 64,
-        )
-    ):
-        pmeta = jnp.where(lane == i, col[:, None], pmeta)
-    pmeta = pmeta.astype(jnp.float32).reshape(pieces, GROUP, 128)
-    normed_blocks = p["normed"].reshape(resp_local, devices, cols).transpose(1, 0, 2)
-    reward_lane = jnp.arange(128, dtype=jnp.int32)[None, :] - me * resp_local
-    reward_row = jnp.sum(
-        jnp.where(
-            reward_lane == jnp.arange(resp_local, dtype=jnp.int32)[:, None],
-            p["own_reward"][:, None], 0.0,
-        ),
-        axis=0,
-    )
-    fm = jnp.concatenate(
-        [
-            jnp.broadcast_to(reward_row[None, None, :], (devices, 1, 128)),
-            codes.astype(jnp.float32),
-            lane_pad(jnp.broadcast_to(over.astype(jnp.float32)[None, :], (devices, devices)), 128),
-            jnp.zeros((devices, 1, 128), jnp.float32),
-            jnp.pad(normed_blocks, ((0, 0), (0, 4 - resp_local), (0, 128 - cols))),
-        ],
-        axis=1,
-    )
+    shard_rows = VOCAB // args[-1].shape[0]
     rows_in, packed, where, slot_info, head, flag = relay_exchange(
-        fm, outgoing, pmeta, p["chosen_index"][:, None], p["rejected_index"][:, None],
-        n_grp, n_dev, p["shard_rows"] // BLOCKS,
+        args, n_grp, n_dev, shard_rows // BLOCKS
     )
 
     def relayed(operands):
@@ -785,13 +855,13 @@
 
         def spread(o):
             return place_all(
-                p["shard_rows"], o[0], o[3][:, 0].reshape(-1).astype(jnp.int32),
+                shard_rows, o[0], o[3][:, 0].reshape(-1).astype(jnp.int32),
                 o[3][:, 1].reshape(-1),
             )
 
         return lax.cond(
             flag[1, 0] <= 0.0,
-            lambda o: place_packed(p["shard_rows"], o[2], o[1]),
+            lambda o: place_packed(shard_rows, o[2], o[1]),
             spread,
             (rows, packed, where, slot_info),
         )
@@ -799,10 +869,10 @@
     owned = lax.cond(
         flag[0, 0] <= 0.0,
         relayed,
-        lambda operands: plain_finish(p, n_dev)[0],
+        lambda operands: plain_finish(prepare(*args), n_dev)[0],
         (rows_in, packed, where, slot_info, flag),
     )
-    return owned, head[0, :cols]
+    return owned, head.reshape(-1)
 
 
 def solution(mesh):

time: 170 us -> 150 us (0.88)
  other arithmetic: 8.1 us -> 0 us
  matrix products: 8.02 us -> 0 us
  local copies, waits for them, and re-layouts: 6.6 us -> 1.54 us
    dot_general x2 -> x0, matrix products: 8.02 us -> none  [the longest x1 7.74 us: relay_local(): jnp.dot(slot_match.astype(jnp.bfloat16), p['sens'], preferred_element_typ...]
    reduce_sum x9 -> x0, other arithmetic: 4.15 us -> none  [the longest x1 1.01 us: prepare(): own_reward = jnp.sum(normed * reward_head, axis=-1)]
    broadcast_in_dim x4 -> x0, local copies, waits for them, and re-layouts: 2.71 us -> none  [the longest x1 1.35 us: relay_local(): p['rejected_index'][:, None]]
where the time goes in v4:
time: 150 us; the launch traced here: 149 us
  Pallas kernels  145 us (97%)
  local copies, waits for them, and re-layouts  1.54 us (1%)
    pallas_call x1, Pallas kernels, relay_exchange(): pl.pallas_call(functools.partial(relay_kernel, n_grp, n_dev, block_rows),...  130 us
    pallas_call x1, Pallas kernels, place_packed(): pl.pallas_call(place_kernel, out_shape=jax.ShapeDtypeStruct((shard_rows,...  14.9 us

profile of v4, /device:TPU:11, one launch (start us, length us, event | category | flops | bytes accessed | tf_op | source)
XLA Modules:
  0.0 149.1 jit_solution(844277396936819874)
XLA Ops:
  0.6 130.5 %shard_map.104 = (bf16[896,4096]{1,0:T(8,128)(2,1)}, bf16[768,4096]{1,0:T(8,128)(2,1)}, f32[8,768]{1,0:T(8,128)S(1)}, f32[7,8,128]{2,1,0:T(8,128)S(1)}, f32[1,128]{1,0:T(1,128)}, /*index=5*/f32[8,128]{1,0:T(8,128)S(1)}) custom-call(s32[4,128]{1,0:T(4,128)} %ids_ref.1, bf16[512,4096]{1,0:T(8,128)(2,1)} %bitcast.50, bf16[4,4096]{1,0:T(4,128)(2,1)} %hidden_ref.1, ...), custom_call_target="tpu_custom_call" | custom-call | tf_op jit(solution)/shard_map/pallas_call | solution.py:610
  131.1 0.5 slice.21
  132.3 0.0 copy-start.2
  132.3 16.2 %conditional.2 = (bf16[4008,4096]{1,0:T(8,128)(2,1)}) conditional(s32[]{:T(128)} %bitcast.15, (s32[4]{0:T(128)}, s32[4,128]{1,0:T(4,128)}, s32[32]{0:T(128)}, bf16[4,4096]{1,0:T(4,128)(2,1)}, f32[4096]{0:T(1024)}, /*index=5*/f32[4096]{0:T(1024)}, bf16[4,128,4096]{2,1,0:T(8,128)(2,1)}, s32[64]{0:T(128)}, s32[64]{0:T(128)}) %tuple.20, ...), branch_computations={%region_0.9_spmd, %region_9.12_spmd} | conditional | flops 37973413888 | bytes 54417232 | solution.py:869
  132.5 0.5 slice.19
  133.7 14.9 %conditional = (bf16[4008,4096]{1,0:T(8,128)(2,1)}) conditional(s32[]{:T(128)} %bitcast.11, (f32[7,8,128]{2,1,0:T(8,128)S(1)}, bf16[896,4096]{1,0:T(8,128)(2,1)}) %tuple.14, (f32[8,768]{1,0:T(8,128)S(1)}, bf16[768,4096]{1,0:T(8,128)(2,1)}) %tuple.15), branch_computations={%region_10.10_spmd, %region_11.11_spmd} | conditional | flops 29449867264 | bytes 40195080 | solution.py:862
  133.7 14.9 %branch_1_fun.1 = bf16[4008,4096]{1,0:T(8,128)(2,1)} custom-call(f32[8,768]{1,0:T(8,128)S(1)} %get-tuple-element.55.where_ref, bf16[768,4096]{1,0:T(8,128)(2,1)} %get-tuple-element.56.packed_ref), custom_call_target="tpu_custom_call" | custom-call | tf_op jit(solution)/shard_map/cond/branch_1_fun/cond/branch_1_fun/pallas_call | solution.py:706
  148.6 0.0 copy-done.2
  148.6 0.5 copy.20
Async XLA Ops:
  132.3 16.3 %copy-start.2 = (f32[1,128]{1,0:T(1,128)S(1)}, f32[1,128]{1,0:T(1,128)}, u32[]{:S(2)}) copy-start(f32[1,128]{1,0:T(1,128)} %get-tuple-element.75) | copy-start | bytes 1540

commit v5 on v4

--- a/solution.py
+++ b/solution.py
@@ -113,11 +113,11 @@
 
 def relay_kernel(n_grp, n_dev, block_rows, ids_ref, sens_ref, hidden_ref, length_ref, gain_ref,
                  weight_ref, chosen_ref, rejected_ref, owner_ref,
-                 rows_out, packed_out, where_out, slot_out, head_out, flag_out,
+                 rows_out, packed, where_out, slot_out, head_out, flag_out,
                  sens_v, select, slots_v, pout, fm_out, pmeta_out,
-                 rin, fin, fm_in, pin, pmeta_in, fwd, fwd_meta, fmeta_in, picks, scales, packed,
+                 rin, fin, fm_in, pin, pmeta_in, fwd, fwd_meta, fmeta_in, picks, scales,
                  sens_sems, fm_sems, near_sems, far_sems, piece_sems, pm_sems, fwd_sems,
-                 fwdm_sems, save_sems, pack_sems):
+                 fwdm_sems, save_sems):
     g = lax.axis_index("grp")
     v = lax.axis_index("dev")
     hd = n_dev // 2
@@ -321,7 +321,7 @@
     def fwd_copies(k):
         to = partner(k, half)
         return [
-            remote(fwd.at[k], fin.at[k], fwd_sems.at[0, k], fwd_sems.at[1, k], to),
+            remote(fwd.at[k], fin.at[pl.ds(k * FWD, FWD)], fwd_sems.at[0, k], fwd_sems.at[1, k], to),
             remote(fwd_meta.at[k], fmeta_in.at[k], fwdm_sems.at[0, k], fwdm_sems.at[1, k], to),
         ]
 
@@ -382,7 +382,7 @@
         out = lax.dot_general(place, rows, contract, preferred_element_type=f32)
         out = out.reshape(local_n, FWD, CHUNK).astype(jnp.bfloat16)
         fwd[:, :, cols] = out
-        fin[0, :, cols] = out[0]
+        fin[pl.ds(0, FWD), cols] = out[0]
         return carry
 
     lax.fori_loop(0, width // CHUNK, gather, 0)
@@ -480,7 +480,7 @@
         ok = live & (rank_b < WINDOW)
         pos = jnp.where(ok, block * WINDOW + rank_b, -1)
         pick = jnp.where(packed_id == pos, 1.0, 0.0)
-        picks[i] = pick.astype(jnp.bfloat16)
+        picks[i // 2, :, pl.ds(i % 2 * 128, 128)] = pick.astype(jnp.bfloat16)
         scale = jnp.sum(jnp.where(resp_id == resp, grad_col, 0.0), axis=0, keepdims=True)
         scale = jnp.where(live, scale, 0.0)
         got = jnp.sum(pick * scale, axis=1, keepdims=True)
@@ -512,10 +512,8 @@
     def pack(seg, first):
         def col(c, carry):
             cols = pl.ds(pl.multiple_of(c * CHUNK, CHUNK), CHUNK)
-            got = jnp.dot(picks[2 * seg], rin[pl.ds(seg * 256, 128), cols],
+            got = jnp.dot(picks[seg], rin[pl.ds(seg * 256, 256), cols],
                           preferred_element_type=f32)
-            got = got + jnp.dot(picks[2 * seg + 1], rin[pl.ds(seg * 256 + 128, 128), cols],
-                                preferred_element_type=f32)
             got = (scales[seg] * got).astype(jnp.bfloat16)
             packed[:, cols] = got if first else packed[:, cols] + got
             return carry
@@ -570,27 +568,16 @@
     filled, worst, found, got = index_tile(6, target, meta_rows[3:4], filled, worst, found)
     scales[3] = got
 
-    def pack_out(c):
-        cols = pl.ds(c * CHUNK, CHUNK)
-        return pltpu.make_async_copy(packed.at[:, cols], packed_out.at[:, cols], pack_sems.at[c])
-
     for c in range(width // CHUNK):
         cols = pl.ds(c * CHUNK, CHUNK)
-        rows = fin[:, :, cols].astype(f32).reshape(128, CHUNK)
-        got = jnp.dot(picks[6].astype(f32), rows, preferred_element_type=f32)
+        got = jnp.dot(picks[3, :, pl.ds(0, 128)], fin[:, cols], preferred_element_type=f32)
         packed[:, cols] = packed[:, cols] + (scales[3] * got).astype(jnp.bfloat16)
-        pack_out(c).start()
-    fwd_save = []
-    for k in range(local_n):
-        fwd_save.append(save(3 + k, fin.at[k], direct + k * FWD, FWD))
-        fwd_save[-1].start()
+    saves.append(save(3, fin, direct, local_n * FWD))
+    saves[3].start()
     where_out[...] = found[0:1] * 64.0 + found[1:2] - 1.0 + jnp.zeros((8, total), f32)
-    flag_out[0:1, :] = jnp.broadcast_to(excess, (1, 128))
-    flag_out[1:8, :] = jnp.broadcast_to(worst - WINDOW, (7, 128))
-    for cp in saves + fwd_save:
+    flag_out[...] = jnp.where(excess > 0.0, 2, jnp.where(worst > WINDOW, 1, 0))
+    for cp in saves:
         cp.wait()
-    for c in range(width // CHUNK):
-        pack_out(c).wait()
 
 
 def relay_exchange(args, n_grp, n_dev, block_rows):
@@ -615,10 +602,10 @@
             jax.ShapeDtypeStruct((8, total), f32),
             jax.ShapeDtypeStruct((rows // 128, 8, 128), f32),
             jax.ShapeDtypeStruct((1, 128), f32),
-            jax.ShapeDtypeStruct((8, 128), f32),
+            jax.ShapeDtypeStruct((1, 1), jnp.int32),
         ),
         in_specs=[vmem, anyspec, vmem, smem, vmem, vmem, smem, smem, smem],
-        out_specs=(anyspec, anyspec, vmem, vmem, vmem, vmem),
+        out_specs=(anyspec, vmem, vmem, vmem, vmem, vmem),
         scratch_shapes=[
             pltpu.VMEM((width // CHUNK, resp_local * block_len, CHUNK), bf16),
             pltpu.VMEM((direct + 48, resp_local * block_len), bf16),
@@ -627,16 +614,15 @@
             pltpu.VMEM((n, 8, 128), f32),
             pltpu.VMEM((pieces, GROUP, 128), f32),
             pltpu.VMEM((direct, width), bf16),
-            pltpu.VMEM((local_n, FWD, width), bf16),
+            pltpu.VMEM((local_n * FWD, width), bf16),
             pltpu.VMEM((n, 8, 128), f32),
             pltpu.VMEM((pieces, GROUP, width), bf16),
             pltpu.VMEM((pieces, GROUP, 128), f32),
             pltpu.VMEM((local_n, FWD, width), bf16),
             pltpu.VMEM((local_n, FWD, 128), f32),
             pltpu.VMEM((local_n, FWD, 128), f32),
-            pltpu.VMEM((rows // 128, total, 128), bf16),
+            pltpu.VMEM((4, total, 256), bf16),
             pltpu.VMEM((4, total, 1), f32),
-            pltpu.VMEM((total, width), bf16),
             sem((width // CHUNK,)),
             sem((2, n)),
             sem((2, local_n)),
@@ -645,17 +631,16 @@
             sem((2, pieces)),
             sem((2, local_n)),
             sem((2, local_n)),
-            sem((3 + local_n,)),
-            sem((width // CHUNK,)),
+            sem((4,)),
         ],
         compiler_params=pltpu.CompilerParams(
-            collective_id=0, has_side_effects=True, vmem_limit_bytes=56 * 1024 * 1024
+            collective_id=0, has_side_effects=True, vmem_limit_bytes=46 * 1024 * 1024
         ),
     )(ids, sens.reshape(-1, width), hidden, lengths, gain[None, :], weight[None, :], chosen,
       rejected, owner)
 
 
-def place_kernel(where_ref, packed_ref, out_ref, src, onehot, outbuf, in_sems, out_sems):
+def place_kernel(where_ref, packed_ref, out_ref, onehot, outbuf, out_sems):
     total, width = packed_ref.shape
     shard_rows = out_ref.shape[0]
     block_rows = shard_rows // BLOCKS
@@ -663,11 +648,6 @@
     chunks = width // CHUNK
     slots = outbuf.shape[0]
 
-    def fetch(c):
-        return pltpu.make_async_copy(
-            packed_ref.at[:, pl.ds(c * CHUNK, CHUNK)], src.at[c], in_sems.at[c]
-        )
-
     def put(b, c, slot):
         return pltpu.make_async_copy(
             outbuf.at[slot, pl.ds(0, block_rows)],
@@ -675,20 +655,16 @@
             out_sems.at[slot],
         )
 
-    for c in range(chunks):
-        fetch(c).start()
     for b in range(BLOCKS):
         row_id = lax.broadcasted_iota(jnp.int32, (padded, WINDOW), 0) + b * block_rows
         target = where_ref[0:1, pl.ds(b * WINDOW, WINDOW)].astype(jnp.int32)
         onehot[...] = jnp.where(row_id == target, 1.0, 0.0).astype(jnp.bfloat16)
         for c in range(chunks):
             step = b * chunks + c
-            if b == 0:
-                fetch(c).wait()
             if step >= slots:
                 put((step - slots) // chunks, (step - slots) % chunks, step % slots).wait()
             outbuf[step % slots] = jnp.dot(
-                onehot[...], src[c, pl.ds(b * WINDOW, WINDOW), :],
+                onehot[...], packed_ref[pl.ds(b * WINDOW, WINDOW), pl.ds(c * CHUNK, CHUNK)],
                 preferred_element_type=jnp.float32,
             ).astype(jnp.bfloat16)
             put(b, c, step % slots).start()
@@ -706,16 +682,14 @@
     return pl.pallas_call(
         place_kernel,
         out_shape=jax.ShapeDtypeStruct((shard_rows, width), packed.dtype),
-        in_specs=[vmem, anyspec],
+        in_specs=[vmem, vmem],
         out_specs=anyspec,
         scratch_shapes=[
-            pltpu.VMEM((chunks, total, CHUNK), jnp.bfloat16),
             pltpu.VMEM((padded, WINDOW), jnp.bfloat16),
             pltpu.VMEM((4, padded, CHUNK), jnp.bfloat16),
-            pltpu.SemaphoreType.DMA((chunks,)),
             pltpu.SemaphoreType.DMA((4,)),
         ],
-        compiler_params=pltpu.CompilerParams(vmem_limit_bytes=48 * 1024 * 1024),
+        compiler_params=pltpu.CompilerParams(vmem_limit_bytes=40 * 1024 * 1024),
     )(where, packed)
 
 
@@ -851,26 +825,18 @@
     )
 
     def relayed(operands):
-        rows, packed, where, slot_info, flag = operands
-
-        def spread(o):
-            return place_all(
-                shard_rows, o[0], o[3][:, 0].reshape(-1).astype(jnp.int32),
-                o[3][:, 1].reshape(-1),
-            )
-
-        return lax.cond(
-            flag[1, 0] <= 0.0,
-            lambda o: place_packed(shard_rows, o[2], o[1]),
-            spread,
-            (rows, packed, where, slot_info),
-        )
-
-    owned = lax.cond(
-        flag[0, 0] <= 0.0,
-        relayed,
-        lambda operands: plain_finish(prepare(*args), n_dev)[0],
-        (rows_in, packed, where, slot_info, flag),
+        return place_packed(shard_rows, operands[2], operands[1])
+
+    def spread(operands):
+        rows, _, _, info = operands
+        return place_all(
+            shard_rows, rows, info[:, 0].reshape(-1).astype(jnp.int32), info[:, 1].reshape(-1)
+        )
+
+    owned = lax.switch(
+        flag.reshape(()),
+        (relayed, spread, lambda operands: plain_finish(prepare(*args), n_dev)[0]),
+        (rows_in, packed, where, slot_info),
     )
     return owned, head.reshape(-1)
 

time: 150 us -> 145 us (0.967)
  Pallas kernels: 145 us -> 142 us
    pallas_call x1, Pallas kernels: 130 us -> 129 us  [relay_exchange(): pl.pallas_call(functools.partial(relay_kernel, n_grp, n_dev, block_rows),...]
    pallas_call x1, Pallas kernels: 14.9 us -> 13.2 us  [place_packed(): pl.pallas_call(place_kernel, out_shape=jax.ShapeDtypeStruct((shard_rows,...]
where the time goes in v5:
time: 145 us; the launch traced here: 144 us
  Pallas kernels  142 us (98%)
    pallas_call x1, Pallas kernels, relay_exchange(): pl.pallas_call(functools.partial(relay_kernel, n_grp, n_dev, block_rows),...  129 us
    pallas_call x1, Pallas kernels, place_packed(): pl.pallas_call(place_kernel, out_shape=jax.ShapeDtypeStruct((shard_rows,...  13.2 us

profile of v5, /device:TPU:11, one launch (start us, length us, event | category | flops | bytes accessed | tf_op | source)
XLA Modules:
  0.0 143.8 jit_solution(10111611185556563565)
XLA Ops:
  0.6 128.6 %shard_map.104 = (bf16[896,4096]{1,0:T(8,128)(2,1)}, bf16[768,4096]{1,0:T(8,128)(2,1)S(1)}, f32[8,768]{1,0:T(8,128)S(1)}, f32[7,8,128]{2,1,0:T(8,128)S(1)}, f32[1,128]{1,0:T(1,128)S(1)}, /*index=5*/s32[1,1]{1,0:T(1,128)}) custom-call(s32[4,128]{1,0:T(4,128)} %ids_ref.1, bf16[512,4096]{1,0:T(8,128)(2,1)} %bitcast.50, bf16[4,4096]{1,0:T(4,128)(2,1)} %hidden_ref.1, ...), custom_call_target="tpu_custom_call" | custom-call | tf_op jit(solution)/shard_map/pallas_call | solution.py:597
  129.9 13.4 %conditional.1 = (bf16[4008,4096]{1,0:T(8,128)(2,1)}) conditional(s32[]{:T(128)} %bitcast.14, (f32[8,768]{1,0:T(8,128)S(1)}, bf16[768,4096]{1,0:T(8,128)(2,1)S(1)}) %tuple.17, (f32[7,8,128]{2,1,0:T(8,128)S(1)}, bf16[896,4096]{1,0:T(8,128)(2,1)}) %tuple.18, (s32[4]{0:T(128)}, s32[4,128]{1,0:T(4,128)}, s32[32]{0:T(128)}, ...), branch_computations={%region_0.0_spmd, %region_1.0_spmd, %region_2.11_spmd} | conditional | flops 37973413888 | bytes 54417232 | solution.py:836
  130.1 13.2 %branch_0_fun.1 = bf16[4008,4096]{1,0:T(8,128)(2,1)} custom-call(f32[8,768]{1,0:T(8,128)S(1)} %get-tuple-element.15.where_ref, bf16[768,4096]{1,0:T(8,128)(2,1)S(1)} %get-tuple-element.16.packed_ref), custom_call_target="tpu_custom_call" | custom-call | tf_op jit(solution)/shard_map/cond/branch_0_fun/pallas_call | solution.py:682
  143.3 0.5 copy.19
